TPU v7x, 32 devices: a whole 2x2x4 slice. The times are simulated.
32 devices in a mesh: dp: 4 (over x, core), ctx: 8 (over z, y).
Axes of the slice: x: 2, y: 2, z: 4, core: 2. Of those that a mesh axis runs over, the one named last changes fastest.
Arguments:
- tokens: bfloat16 [4096, 1792], P(('dp', 'ctx')), may hold values from -6 to 6
- cotangent: bfloat16 [4096, 1792], P(('dp', 'ctx')), may hold values from -6 to 6
- expert_ids: int32 [4096, 4], P(('dp', 'ctx')), may hold values from 0 to 15, all different within a row; in each aligned block of 128 rows (0 to 127, 128 to 255, ...) at most 40 rows name the same one
- norm_gain: float32 [1792], replicated, may hold values from 0.5 to 1.5
- router_weight: bfloat16 [1792, 16], replicated, may hold values from -0.125 to 0.125
- gate_weight: bfloat16 [16, 1792, 1536], P('ctx', None, 'dp'), may hold values from -0.125 to 0.125
- up_weight: bfloat16 [16, 1792, 1536], P('ctx', None, 'dp'), may hold values from -0.125 to 0.125
- down_weight: bfloat16 [16, 1536, 1792], P('ctx', 'dp'), may hold values from -0.15625 to 0.15625
Outputs:
- grad_tokens: bfloat16 [4096, 1792], P(('dp', 'ctx'))
- grad_gate: bfloat16 [16, 1792, 1536], P('ctx', None, 'dp')
- grad_up: bfloat16 [16, 1792, 1536], P('ctx', None, 'dp')
- grad_down: bfloat16 [16, 1536, 1792], P('ctx', 'dp')
- grad_router: float32 [1792, 16], P(('dp', 'ctx'))
- grad_gain: float32 [1792], P(('dp', 'ctx'))
Inputs may be any that keep to these rules, and one draw needn't show every extreme that they name: `expert_ids`: each row names 4 different experts; among the rows of one device no expert is named more than 40 times.
All inputs are finite; a program needn't handle non-finite values.
Results may differ from a plain program's by a relative error of at most 0.02.
Values may be sent and summed in bfloat16 or wider, within the bound.
No kernel may reach another device: no remote copies, remote signals or barrier semaphores. Data moves between devices by JAX's collectives and lax.ppermute only.
A program may use at most 192 MiB of HBM per device.

v0:
```python
import functools

import jax
import jax.numpy as jnp
from jax import lax
from jax.experimental import pallas as pl
from jax.experimental.pallas import tpu as pltpu
from jax.sharding import PartitionSpec as P


EPSILON = 1e-05
SWISH_SCALE = 1.702
LANES = 128
BF = jnp.bfloat16
F32 = jnp.float32


def dot(a, b, ca=1, cb=0):
    return lax.dot_general(a, b, (((ca,), (cb,)), ((), ())), preferred_element_type=F32)


def vmem(count):
    return [pl.BlockSpec(memory_space=pltpu.VMEM)] * count


def normalize(tokens_ref, gain_ref):
    widened = tokens_ref[...].astype(F32)
    inverse = lax.rsqrt(jnp.mean(widened * widened, axis=1, keepdims=True) + EPSILON)
    scaled = widened * inverse
    gain = gain_ref[...][None, :]
    return inverse, scaled, (scaled * gain).astype(BF), gain


def permutation(labels_ref, count):
    shape = (labels_ref.shape[0], count)
    return (labels_ref[...] == lax.broadcasted_iota(jnp.int32, shape, 1)).astype(F32).astype(BF)


def slot_mask(table_t, first, local, cap, axis):
    rows = table_t.shape[1 - axis]
    shape = (local * cap, rows) if axis == 0 else (rows, local * cap)
    slot = lax.broadcasted_iota(jnp.int32, shape, axis)
    hit = None
    for e in range(local):
        line = table_t[first + e : first + e + 1, :] if axis == 0 else table_t[:, first + e : first + e + 1]
        one = line == (slot - e * cap).astype(F32)
        one = one & (slot >= e * cap) & (slot < (e + 1) * cap)
        hit = one if hit is None else hit | one
    return hit


def head_kernel(local, cap, tokens_ref, cot_ref, ids_ref, labels_ref, gain_ref, router_ref, *outs):
    messages, (rank_ref, gates_ref) = outs[:-2], outs[-2:]
    rows, width = tokens_ref.shape
    _, _, normed, _ = normalize(tokens_ref, gain_ref)
    router = dot(permutation(labels_ref, router_ref.shape[0]), router_ref[...]).astype(BF)
    logits = dot(router, normed, 1, 1)
    member = None
    for k in range(ids_ref.shape[0]):
        one = ids_ref[k : k + 1, :] == labels_ref[...]
        member = one if member is None else member | one
    lifted = jnp.where(member, jnp.exp(jnp.where(member, logits, 0.0)), 0.0)
    gates_t = lifted / jnp.sum(lifted, axis=0, keepdims=True)
    upto = lax.broadcasted_iota(jnp.int32, (rows, rows), 0) <= lax.broadcasted_iota(jnp.int32, (rows, rows), 1)
    rank_t = dot(member.astype(F32).astype(BF), upto.astype(F32).astype(BF)) - 1.0
    rank_t = jnp.where(member, rank_t, -1.0)
    rank_ref[...] = rank_t
    gates_ref[...] = gates_t
    cot = cot_ref[...]
    for s, out in enumerate(messages):
        hit = slot_mask(rank_t, s * local, local, cap, 0)
        slot = lax.broadcasted_iota(jnp.int32, hit.shape, 0)
        spread = None
        for e in range(local):
            line = gates_t[s * local + e : s * local + e + 1, :]
            part = jnp.where(hit & (slot >= e * cap) & (slot < (e + 1) * cap), line, 0.0)
            spread = part if spread is None else spread + part
        weight = jnp.sum(spread, axis=1, keepdims=True)
        pick = hit.astype(F32).astype(BF)
        out[:, :width] = dot(pick, normed).astype(BF)
        out[:, width:] = (dot(pick, cot) * weight).astype(BF)


def expert_kernel(width, near_ref, far_ref, gate_ref, up_ref, down_ref, *outs):
    gate, up, down = gate_ref[0], up_ref[0], down_ref[0]
    ff = gate.shape[1]
    for rows_ref, (back_ref, hidden_ref, pre_ref) in ((near_ref, outs[:3]), (far_ref, outs[3:])):
        rows = rows_ref[0, :, :width]
        gate_pre = dot(rows, gate)
        up_one = dot(rows, up) + 1.0
        grad = dot(rows_ref[0, :, width:], down, 1, 1)
        squash = jax.nn.sigmoid(SWISH_SCALE * gate_pre)
        swish = gate_pre * squash
        hidden = (swish * up_one).astype(BF)
        score = jnp.sum(grad * hidden.astype(F32), axis=1, keepdims=True)
        slope = squash + SWISH_SCALE * swish * (1.0 - squash)
        pre_gate = (grad * up_one * slope).astype(BF)
        pre_up = (grad * swish).astype(BF)
        hidden_ref[0] = hidden
        pre_ref[0, :, :ff] = pre_gate
        pre_ref[0, :, ff:] = pre_up
        back = dot(pre_gate, gate, 1, 1) + dot(pre_up, up, 1, 1)
        back_ref[0, :, :width] = back.astype(BF)
        lane = lax.broadcasted_iota(jnp.int32, (rows.shape[0], LANES), 1)
        back_ref[0, :, width:] = jnp.where(lane == 0, score, 0.0).astype(BF)


def weight_kernel(count, *refs):
    rows, ups = refs[:count], refs[count : 2 * count]
    hiddens, pres = refs[2 * count : 3 * count], refs[3 * count : 4 * count]
    gate_out, up_out, down_out = refs[-3:]
    ff = gate_out.shape[2]
    both = sum(dot(r[0], p[0], 0, 0) for r, p in zip(rows, pres))
    gate_out[0] = both[:, :ff].astype(BF)
    up_out[0] = both[:, ff:].astype(BF)
    down_out[0] = sum(dot(h[0], u[0], 0, 0) for h, u in zip(hiddens, ups)).astype(BF)


def tail_kernel(local, cap, experts, shard, count, *refs):
    pieces = refs[:count]
    rank_ref, gates_ref, tokens_ref, cot_ref, labels_ref, gain_ref, router_ref = refs[count : count + 7]
    grad_ref, part_ref, score_ref = refs[count + 7 :]
    width = tokens_ref.shape[1]
    rank_t = rank_ref[...]
    rank = rank_t.T
    inverse, scaled, normed, gain = normalize(tokens_ref, gain_ref)
    router = dot(permutation(labels_ref, experts), router_ref[...]).astype(BF)
    score_ref[...] = jnp.zeros(score_ref.shape, F32)
    back = None
    for s, piece in enumerate(pieces):
        pick = slot_mask(rank, s * local, local, cap, 1).astype(F32).astype(BF)
        part = dot(pick, piece[:, :width])
        back = part if back is None else back + part
        column = piece[:, width : width + LANES].astype(F32)[:, :1]
        hit = slot_mask(rank_t, s * local, local, cap, 0)
        slot = lax.broadcasted_iota(jnp.int32, hit.shape, 0)
        for e in range(local):
            mine = hit & (slot >= e * cap) & (slot < (e + 1) * cap)
            score_ref[s * local + e : s * local + e + 1, :] = jnp.sum(
                jnp.where(mine, column, 0.0), axis=0, keepdims=True
            )
    score = score_ref[...]
    mixed = jnp.sum(score, axis=0, keepdims=True)
    grad_logits = jnp.where(rank_t >= 0.0, score - gates_ref[...] * mixed, 0.0)
    grad_normed = back + dot(grad_logits.T.astype(BF), router)
    natural = dot(permutation(labels_ref, LANES), grad_logits.astype(BF), 0, 0)
    part_t = dot(natural.astype(BF), normed)
    gain_part = jnp.sum(grad_normed * scaled, axis=0, keepdims=True)
    wide = part_ref.shape[1]
    line = lax.broadcasted_iota(jnp.int32, (wide, width), 0)
    part = jnp.where(line == experts, gain_part, part_t[:wide])
    part_ref[...] = jnp.zeros(part_ref.shape, F32)
    for d in range(part_ref.shape[0]):
        part_ref[d, :, :shard] = part[:, d * shard : (d + 1) * shard]
    grad_scaled = grad_normed * gain
    correction = jnp.mean(grad_scaled * scaled, axis=1, keepdims=True)
    grad_ref[...] = (
        cot_ref[...].astype(F32) + inverse * (grad_scaled - scaled * correction)
    ).astype(BF)


def body(tokens, cotangent, expert_ids, norm_gain, router_weight, gate_weight, up_weight, down_weight):
    n_ctx, n_dp = lax.axis_size("ctx"), lax.axis_size("dp")
    me = lax.axis_index("ctx")
    local, width, ff = gate_weight.shape
    experts = router_weight.shape[1]
    rows_here, picks = expert_ids.shape
    cap = max(2, rows_here * picks * 5 // (4 * experts))
    slots = local * cap
    wide = width + LANES
    labels = jnp.arange(experts, dtype=jnp.int32)
    labels = ((labels // local) ^ me) * local + labels % local
    labels = jnp.pad(labels, (0, LANES - experts), constant_values=-1)[:, None]
    router = router_weight.T
    limit = pltpu.CompilerParams(vmem_limit_bytes=56 * 1024 * 1024)

    *messages, rank, gates = pl.pallas_call(
        functools.partial(head_kernel, local, cap),
        out_shape=[jax.ShapeDtypeStruct((slots, 2 * width), BF)] * n_ctx
        + [jax.ShapeDtypeStruct((rows_here, LANES), F32)] * 2,
        in_specs=vmem(6),
        out_specs=vmem(n_ctx + 2),
        compiler_params=limit,
        name="head",
    )(tokens, cotangent, expert_ids.T, labels, norm_gain, router)

    def across(value, s):
        return lax.ppermute(value, "ctx", [(i, i ^ s) for i in range(n_ctx)])

    def chip(value):
        return lax.ppermute(value, "dp", [(i, i ^ 2) for i in range(n_dp)])

    def core(value):
        return lax.ppermute(value, "dp", [(i, i ^ 1) for i in range(n_dp)])

    half, quarter = n_ctx // 2, n_ctx // 4
    groups = (range(half), range(half, half + quarter), range(half + quarter, n_ctx))
    arrived = {s: across(messages[s], s) if s else messages[s] for s in range(n_ctx)}
    crossed = {s: chip(arrived[s]) for s in range(n_ctx)}

    def expert_pass(near, far):
        rows = near.shape[1]
        spec = lambda *shape: pl.BlockSpec((1, *shape), lambda e: (e, 0, 0))
        outs = ((rows, wide), (rows, ff), (rows, 2 * ff)) * 2
        flops = 2 * 2 * local * rows * width * ff * 5
        return pl.pallas_call(
            functools.partial(expert_kernel, width),
            grid=(local,),
            in_specs=[spec(rows, 2 * width)] * 2 + [spec(width, ff)] * 2 + [spec(ff, width)],
            out_specs=[spec(*o) for o in outs],
            out_shape=[jax.ShapeDtypeStruct((local, *o), BF) for o in outs],
            compiler_params=limit,
            cost_estimate=pl.CostEstimate(flops=flops, bytes_accessed=16 * rows * width, transcendentals=0),
            name="expert",
        )(near, far, gate_weight, up_weight, down_weight)

    done = []
    for group in groups:
        parts = [arrived[s] for s in group] + [crossed[s] for s in group]
        near = jnp.concatenate([p.reshape(local, cap, 2 * width) for p in parts], axis=1)
        far = core(near)
        done.append((near, far, *expert_pass(near, far)))

    returned = {}
    for g in (1, 2, 0):
        group = groups[g]
        size = len(group) * cap
        back_near, back_far = done[g][2], done[g][5]
        other = core(back_far)
        leave = (back_near[:, size:].astype(F32) + other[:, size:].astype(F32)).astype(BF)
        came = chip(leave)
        for i, s in enumerate(group):
            cut = slice(i * cap, (i + 1) * cap)
            final = back_near[:, cut].astype(F32) + other[:, cut].astype(F32) + came[:, cut].astype(F32)
            final = final.astype(BF).reshape(slots, wide)
            returned[s] = across(final, s) if s else final

    near_rows = [d[0] for d in done] + [d[1] for d in done]
    hiddens = [d[3] for d in done] + [d[6] for d in done]
    pres = [d[4] for d in done] + [d[7] for d in done]
    count = len(near_rows)
    steps = 2
    tile = width // steps
    total = sum(r.shape[1] for r in near_rows)

    def weights(step):
        row_specs = [pl.BlockSpec((1, r.shape[1], tile), lambda e: (e, 0, step)) for r in near_rows]
        up_specs = [pl.BlockSpec((1, r.shape[1], tile), lambda e: (e, 0, step + steps)) for r in near_rows]
        hid_specs = [pl.BlockSpec((1, r.shape[1], ff), lambda e: (e, 0, 0)) for r in near_rows]
        pre_specs = [pl.BlockSpec((1, r.shape[1], 2 * ff), lambda e: (e, 0, 0)) for r in near_rows]
        carry = list(grads) if step else []
        return pl.pallas_call(
            functools.partial(weight_kernel, count),
            grid=(local,),
            in_specs=row_specs + up_specs + hid_specs + pre_specs + [pl.BlockSpec(memory_space=pl.ANY)] * len(carry),
            out_specs=[pl.BlockSpec((1, tile, ff), lambda e: (e, step, 0))] * 2
            + [pl.BlockSpec((1, ff, tile), lambda e: (e, 0, step))],
            out_shape=[jax.ShapeDtypeStruct((local, width, ff), BF)] * 2
            + [jax.ShapeDtypeStruct((local, ff, width), BF)],
            input_output_aliases={4 * count + i: i for i in range(len(carry))},
            compiler_params=limit,
            cost_estimate=pl.CostEstimate(
                flops=2 * local * total * tile * ff * 3, bytes_accessed=local * total * 4 * tile, transcendentals=0
            ),
        )(*near_rows, *near_rows, *hiddens, *pres, *carry)

    grads = None
    for step in range(steps):
        grads = weights(step)
    gate_grad, up_grad, down_grad = grads

    devices = n_dp * n_ctx
    shard = width // devices
    lines = -(-(experts + 1) // 8) * 8
    grad_input, part = pl.pallas_call(
        functools.partial(tail_kernel, local, cap, experts, shard, n_ctx),
        out_shape=[
            jax.ShapeDtypeStruct((rows_here, width), BF),
            jax.ShapeDtypeStruct((devices, lines, LANES), F32),
        ],
        in_specs=vmem(n_ctx + 7),
        out_specs=vmem(2),
        scratch_shapes=[pltpu.VMEM((LANES, rows_here), F32)],
        compiler_params=limit,
        name="tail",
    )(*[returned[s] for s in range(n_ctx)], rank, gates, tokens, cotangent, labels, norm_gain, router)
    part = jnp.sum(lax.all_to_all(part, ("dp", "ctx"), 0, 0, tiled=True), axis=0)
    return (grad_input, gate_grad, up_grad, down_grad, part[:experts, :shard].T, part[experts, :shard])


def solution(mesh):
    return jax.shard_map(
        body,
        mesh=mesh,
        in_specs=(
            P(("dp", "ctx"), None),
            P(("dp", "ctx"), None),
            P(("dp", "ctx"), None),
            P(),
            P(),
            P("ctx", None, "dp"),
            P("ctx", None, "dp"),
            P("ctx", "dp", None),
        ),
        out_specs=(
            P(("dp", "ctx"), None),
            P("ctx", None, "dp"),
            P("ctx", None, "dp"),
            P("ctx", "dp", None),
            P(("dp", "ctx"), None),
            P(("dp", "ctx")),
        ),
        check_vma=False,
    )
```

profile of v0, /device:TPU:0, one launch (start us, length us, event | category | flops | bytes accessed | tf_op | source)
XLA Modules:
  0.0 354.6 jit_solution(9104573336733029605)
XLA Ops:
  1.4 4.2 %head.1 = (bf16[80,3584]{1,0:T(8,128)(2,1)}, bf16[80,3584]{1,0:T(8,128)(2,1)}, bf16[80,3584]{1,0:T(8,128)(2,1)}, bf16[80,3584]{1,0:T(8,128)(2,1)}, bf16[80,3584]...) custom-call(bf16[128,1792]{1,0:T(8,128)(2,1)} %refs_10_.1, ...), custom_call_target="tpu_custom_call" | custom-call | tf_op jit(solution)/shard_map/head/pallas_call | solution.py:177
  5.6 3.0 collective-permute-start
  10.2 1.9 collective-permute-start.3
  13.2 8.6 %collective-permute-done = bf16[80,3584]{1,0:T(8,128)(2,1)S(1)} collective-permute-done((bf16[80,3584]{1,0:T(8,128)(2,1)}, bf16[80,3584]{1,0:T(8,128)(2,1)S(1)}, u32[]{:S(2)}, u32[]{:S(2)}) %collective-permute-start) | collective-permute-done | bytes 573472 | tf_op jit(solution)/shard_map/ppermute | solution.py:188
  21.9 2.8 collective-permute-done.1
  26.3 9.1 %collective-permute-done.2 = bf16[80,3584]{1,0:T(8,128)(2,1)S(1)} collective-permute-done((bf16[80,3584]{1,0:T(8,128)(2,1)}, bf16[80,3584]{1,0:T(8,128)(2,1)S(1)}, u32[]{:S(2)}, u32[]{:S(2)}) %collective-permute-start.2) | collective-permute-done | bytes 573472 | tf_op jit(solution)/shard_map/ppermute | solution.py:188
  37.7 13.7 %collective-permute-done.5 = bf16[80,3584]{1,0:T(8,128)(2,1)S(1)} collective-permute-done((bf16[80,3584]{1,0:T(8,128)(2,1)S(1)}, bf16[80,3584]{1,0:T(8,128)(2,1)S(1)}, u32[]{:S(2)}, u32[]{:S(2)}) %collective-permute-start.5) | collective-permute-done | bytes 573472 | tf_op jit(solution)/shard_map/ppermute | solution.py:191
  51.4 10.3 %collective-permute-done.6 = bf16[80,3584]{1,0:T(8,128)(2,1)S(1)} collective-permute-done((bf16[80,3584]{1,0:T(8,128)(2,1)S(1)}, bf16[80,3584]{1,0:T(8,128)(2,1)S(1)}, u32[]{:S(2)}, u32[]{:S(2)}) %collective-permute-start.6) | collective-permute-done | bytes 573472 | tf_op jit(solution)/shard_map/ppermute | solution.py:191
  61.8 2.6 collective-permute-start.13
  65.7 3.6 %collective-permute-start.22 = (bf16[80,3584]{1,0:T(8,128)(2,1)S(1)}, bf16[80,3584]{1,0:T(8,128)(2,1)S(1)}, u32[]{:S(2)}, u32[]{:S(2)}) collective-permute-start(bf16[80,3584]{1,0:T(8,128)(2,1)S(1)} %copy-done.13), channel_id=1, source_target_pairs={{0,6},{1,7},{2,4},{3,5},{4,2},{5,3},{6,0},{7,1},{8,14},{9,15},{10,... | collective-permute-start | bytes 1720328 | tf_op jit(solution)/shard_map/ppermute | solution.py:188
  69.5 58.2 %collective-permute-done.13 = bf16[80,3584]{1,0:T(8,128)(2,1)S(1)} collective-permute-done((bf16[80,3584]{1,0:T(8,128)(2,1)S(1)}, bf16[80,3584]{1,0:T(8,128)(2,1)S(1)}, u32[]{:S(2)}, u32[]{:S(2)}) %collective-permute-start.13) | collective-permute-done | bytes 573472 | tf_op jit(solution)/shard_map/ppermute | solution.py:188
  129.2 11.8 %collective-permute-done.14 = bf16[80,3584]{1,0:T(8,128)(2,1)S(1)} collective-permute-done((bf16[80,3584]{1,0:T(8,128)(2,1)S(1)}, bf16[80,3584]{1,0:T(8,128)(2,1)S(1)}, u32[]{:S(2)}, u32[]{:S(2)}) %collective-permute-start.14) | collective-permute-done | bytes 573472 | tf_op jit(solution)/shard_map/ppermute | solution.py:188
  144.4 12.3 %collective-permute-done.16 = bf16[80,3584]{1,0:T(8,128)(2,1)S(1)} collective-permute-done((bf16[80,3584]{1,0:T(8,128)(2,1)S(1)}, bf16[80,3584]{1,0:T(8,128)(2,1)S(1)}, u32[]{:S(2)}, u32[]{:S(2)}) %collective-permute-start.16) | collective-permute-done | bytes 573472 | tf_op jit(solution)/shard_map/ppermute | solution.py:191
  157.0 12.0 %collective-permute-done.24 = bf16[80,3584]{1,0:T(8,128)(2,1)S(1)} collective-permute-done((bf16[80,3584]{1,0:T(8,128)(2,1)S(1)}, bf16[80,3584]{1,0:T(8,128)(2,1)S(1)}, u32[]{:S(2)}, u32[]{:S(2)}) %collective-permute-start.24) | collective-permute-done | bytes 573472 | tf_op jit(solution)/shard_map/ppermute | solution.py:191
  169.0 10.3 %collective-permute-done.25 = bf16[80,3584]{1,0:T(8,128)(2,1)S(1)} collective-permute-done((bf16[80,3584]{1,0:T(8,128)(2,1)S(1)}, bf16[80,3584]{1,0:T(8,128)(2,1)S(1)}, u32[]{:S(2)}, u32[]{:S(2)}) %collective-permute-start.25) | collective-permute-done | bytes 573472 | tf_op jit(solution)/shard_map/ppermute | solution.py:191
  181.0 18.6 %expert.3 = (bf16[2,320,1920]{2,1,0:T(8,128)(2,1)}, bf16[2,320,384]{2,1,0:T(8,128)(2,1)}, bf16[2,320,768]{2,1,0:T(8,128)(2,1)}, bf16[2,320,1920]{2,1,0:T(8,128)(...) custom-call(bf16[2,320,3584]{2,1,0:T(8,128)(2,1)} %copy-done, ...), custom_call_target="tpu_custom_call" | custom-call | flops 8808038400 | bytes 9175040 | tf_op jit(solution)/shard_map/expert/pallas_call | solution.py:206
  200.1 12.6 %expert.4 = (bf16[2,160,1920]{2,1,0:T(8,128)(2,1)}, bf16[2,160,384]{2,1,0:T(8,128)(2,1)}, bf16[2,160,768]{2,1,0:T(8,128)(2,1)}, bf16[2,160,1920]{2,1,0:T(8,128)(...) custom-call(bf16[2,160,3584]{2,1,0:T(8,128)(2,1)} %copy-done.1, ...), custom_call_target="tpu_custom_call" | custom-call | flops 4404019200 | bytes 4587520 | tf_op jit(solution)/shard_map/expert/pallas_call | solution.py:206
  212.8 12.8 %expert.5 = (bf16[2,160,1920]{2,1,0:T(8,128)(2,1)}, bf16[2,160,384]{2,1,0:T(8,128)(2,1)}, bf16[2,160,768]{2,1,0:T(8,128)(2,1)}, bf16[2,160,1920]{2,1,0:T(8,128)(...) custom-call(bf16[2,160,3584]{2,1,0:T(8,128)(2,1)} %pad_maximum_fusion.1.near_ref.refs_2_.refs_8_, ...), custom_call_target="tpu_custom_call" | custom-call | flops 4404019200 | bytes 4587520 | tf_op jit(solution)/shard_map/expert/pallas_call | solution.py:206
  231.8 11.3 %collective-permute-done.19 = bf16[2,80,1920]{2,1,0:T(8,128)(2,1)S(1)} collective-permute-done((bf16[2,80,1920]{2,1,0:T(8,128)(2,1)S(1)}, bf16[2,80,1920]{2,1,0:T(8,128)(2,1)S(1)}, u32[]{:S(2)}, u32[]{:S(2)}) %collective-permute-start.19) | collective-permute-done | bytes 614432 | tf_op jit(solution)/shard_map/ppermute | solution.py:191
  243.3 3.2 collective-permute-start.20
  246.6 35.1 %collective-permute-done.28 = bf16[2,80,1920]{2,1,0:T(8,128)(2,1)S(1)} collective-permute-done((bf16[2,80,1920]{2,1,0:T(8,128)(2,1)S(1)}, bf16[2,80,1920]{2,1,0:T(8,128)(2,1)S(1)}, u32[]{:S(2)}, u32[]{:S(2)}) %collective-permute-start.28) | collective-permute-done | bytes 614432 | tf_op jit(solution)/shard_map/ppermute | solution.py:191
  281.9 4.0 %collective-permute-start.29 = (bf16[80,1920]{1,0:T(8,128)(2,1)S(1)}, bf16[80,1920]{1,0:T(8,128)(2,1)S(1)}, u32[]{:S(2)}, u32[]{:S(2)}) collective-permute-start(bf16[80,1920]{1,0:T(8,128)(2,1)S(1)} %bitcast.55), channel_id=1, source_target_pairs={{0,6},{1,7},{2,4},{3,5},{4,2},{5,3},{6,0},{7,1},{8,14},{9,15},{10,... | collective-permute-start | bytes 921608 | tf_op jit(solution)/shard_map/ppermute | solution.py:188
  286.1 2.4 add_convert_fusion.7
  288.5 2.9 collective-permute-start.12
  292.0 2.2 collective-permute-done.29.refs_6_
  294.3 6.5 %collective-permute-done.30.refs_7_ = bf16[80,1920]{1,0:T(8,128)(2,1)S(1)} collective-permute-done((bf16[80,1920]{1,0:T(8,128)(2,1)S(1)}, bf16[80,1920]{1,0:T(8,128)(2,1)S(1)}, u32[]{:S(2)}, u32[]{:S(2)}) %collective-permute-start.30) | collective-permute-done | bytes 307232 | tf_op jit(solution)/shard_map/ppermute | solution.py:188
  300.8 6.1 %collective-permute-done.11.refs_2_ = bf16[80,1920]{1,0:T(8,128)(2,1)S(1)} collective-permute-done((bf16[80,1920]{1,0:T(8,128)(2,1)S(1)}, bf16[80,1920]{1,0:T(8,128)(2,1)S(1)}, u32[]{:S(2)}, u32[]{:S(2)}) %collective-permute-start.11) | collective-permute-done | bytes 307232 | tf_op jit(solution)/shard_map/ppermute | solution.py:188
  306.9 8.9 %collective-permute-done.12.refs_3_ = bf16[80,1920]{1,0:T(8,128)(2,1)S(1)} collective-permute-done((bf16[80,1920]{1,0:T(8,128)(2,1)S(1)}, bf16[80,1920]{1,0:T(8,128)(2,1)S(1)}, u32[]{:S(2)}, u32[]{:S(2)}) %collective-permute-start.12) | collective-permute-done | bytes 307232 | tf_op jit(solution)/shard_map/ppermute | solution.py:188
  316.6 4.7 %tail.1 = (bf16[128,1792]{1,0:T(8,128)(2,1)}, f32[32,24,128]{2,1,0:T(8,128)}) custom-call(bf16[80,1920]{1,0:T(8,128)(2,1)} %bitcast.32, bf16[80,1920]{1,0:T(8,128)(2,1)} %copy-done.11, bf16[80,1920]{1,0:T(8,128)(2,1)} %copy-done.9, bf16[80,1920]{1,0:T(8,128)(2,1)} %copy-done.10, bf16[80,1920]{1,0:T(8,128)(2,1)} %copy-done.5, bf16[80,1920]{1,0:T(8,128)(2,1)} %copy-done.6, ...), custom_call_target="tpu_custom_call" | custom-call | tf_op jit(solution)/shard_map/tail/pallas_call | solution.py:275
  321.4 4.7 %all-to-all-start = ((f32[32,24,128]{2,1,0:T(8,128)}), f32[32,24,128]{2,1,0:T(8,128)S(1)}, u32[]{:S(2)}, u32[]{:S(2)}) async-start(f32[32,24,128]{2,1,0:T(8,128)} %get-tuple-element.77), calls=%async_computation | async-start | bytes 786432 | tf_op jit(solution)/shard_map/all_to_all | solution.py:287
  326.1 13.6 %shard_map.127 = (bf16[2,1792,384]{2,1,0:T(8,128)(2,1)}, bf16[2,1792,384]{2,1,0:T(8,128)(2,1)}, bf16[2,384,1792]{2,1,0:T(8,128)(2,1)}) custom-call(bf16[2,320,3584]{2,1,0:T(8,128)(2,1)} %copy-done, bf16[2,160,3584]{2,1,0:T(8,128)(2,1)} %copy-done.1, bf16[2,160,3584]{2,1,0:T(8,128)(2,1)} %pad_maximum_fusion.1.near_ref.refs_2_.refs_8_, ...), custom_call_target="tpu_custom_call" | custom-call | flops 5284823040 | bytes 9175040 | tf_op jit(solution)/shard_map/pallas_call | solution.py:252
  339.8 13.7 %shard_map.128 = (bf16[2,1792,384]{2,1,0:T(8,128)(2,1)}, bf16[2,1792,384]{2,1,0:T(8,128)(2,1)}, bf16[2,384,1792]{2,1,0:T(8,128)(2,1)}) custom-call(bf16[2,320,3584]{2,1,0:T(8,128)(2,1)} %copy-done, bf16[2,160,3584]{2,1,0:T(8,128)(2,1)} %copy-done.1, ...), custom_call_target="tpu_custom_call", output_to_operand_aliasing={{0}: (24, {}), {1}: (25, {}), {2}: (26, {})} | custom-call | flops 5284823040 | bytes 9175040 | tf_op jit(solution)/shard_map/pallas_call | solution.py:252
  (93 shorter events, 25.7 us)
Async XLA Ops:
  5.6 16.2 %collective-permute-start = (bf16[80,3584]{1,0:T(8,128)(2,1)}, bf16[80,3584]{1,0:T(8,128)(2,1)S(1)}, u32[]{:S(2)}, u32[]{:S(2)}) collective-permute-start(bf16[80,3584]{1,0:T(8,128)(2,1)} %get-tuple-element.43), channel_id=1, source_target_pairs={{0,1},{1,0},{2,3},{3,2},{4,5},{5,4},{6,7},{7,6},{8,9},{9,8},{10,11... | collective-permute-start | bytes 1720328 | tf_op jit(solution)/shard_map/ppermute | solution.py:188
  8.6 16.1 %collective-permute-start.1 = (bf16[80,3584]{1,0:T(8,128)(2,1)}, bf16[80,3584]{1,0:T(8,128)(2,1)S(1)}, u32[]{:S(2)}, u32[]{:S(2)}) collective-permute-start(bf16[80,3584]{1,0:T(8,128)(2,1)} %get-tuple-element.44), channel_id=1, source_target_pairs={{0,2},{1,3},{2,0},{3,1},{4,6},{5,7},{6,4},{7,5},{8,10},{9,11},{10,... | collective-permute-start | bytes 1720328 | tf_op jit(solution)/shard_map/ppermute | solution.py:188
  10.2 25.1 %collective-permute-start.2 = (bf16[80,3584]{1,0:T(8,128)(2,1)}, bf16[80,3584]{1,0:T(8,128)(2,1)S(1)}, u32[]{:S(2)}, u32[]{:S(2)}) collective-permute-start(bf16[80,3584]{1,0:T(8,128)(2,1)} %get-tuple-element.45), channel_id=1, source_target_pairs={{0,3},{1,2},{2,1},{3,0},{4,7},{5,6},{6,5},{7,4},{8,11},{9,10},{10,... | collective-permute-start | bytes 1720328 | tf_op jit(solution)/shard_map/ppermute | solution.py:188
  10.2 26.9 %collective-permute-start.3 = (bf16[80,3584]{1,0:T(8,128)(2,1)}, bf16[80,3584]{1,0:T(8,128)(2,1)S(1)}, u32[]{:S(2)}, u32[]{:S(2)}) collective-permute-start(bf16[80,3584]{1,0:T(8,128)(2,1)} %get-tuple-element.42), channel_id=1, source_target_pairs={{0,16},{8,24},{16,0},{24,8},{1,17},{9,25},{17,1},{25,9},{2,18},{10... | collective-permute-start | bytes 1720328 | tf_op jit(solution)/shard_map/ppermute | solution.py:191
  24.7 12.9 %collective-permute-start.4 = (bf16[80,3584]{1,0:T(8,128)(2,1)S(1)}, bf16[80,3584]{1,0:T(8,128)(2,1)S(1)}, u32[]{:S(2)}, u32[]{:S(2)}) collective-permute-start(bf16[80,3584]{1,0:T(8,128)(2,1)S(1)} %collective-permute-done), channel_id=1, source_target_pairs={{0,16},{8,24},{16,0},{24,8},{1,17},{9,25},{17,1},{25,9},{2,18},{10... | collective-permute-start | bytes 1720328 | tf_op jit(solution)/shard_map/ppermute | solution.py:191
  35.4 15.9 %collective-permute-start.5 = (bf16[80,3584]{1,0:T(8,128)(2,1)S(1)}, bf16[80,3584]{1,0:T(8,128)(2,1)S(1)}, u32[]{:S(2)}, u32[]{:S(2)}) collective-permute-start(bf16[80,3584]{1,0:T(8,128)(2,1)S(1)} %collective-permute-done.1), channel_id=1, source_target_pairs={{0,16},{8,24},{16,0},{24,8},{1,17},{9,25},{17,1},{25,9},{2,18},{10... | collective-permute-start | bytes 1720328 | tf_op jit(solution)/shard_map/ppermute | solution.py:191
  37.2 24.5 %collective-permute-start.6 = (bf16[80,3584]{1,0:T(8,128)(2,1)S(1)}, bf16[80,3584]{1,0:T(8,128)(2,1)S(1)}, u32[]{:S(2)}, u32[]{:S(2)}) collective-permute-start(bf16[80,3584]{1,0:T(8,128)(2,1)S(1)} %collective-permute-done.2), channel_id=1, source_target_pairs={{0,16},{8,24},{16,0},{24,8},{1,17},{9,25},{17,1},{25,9},{2,18},{10... | collective-permute-start | bytes 1720328 | tf_op jit(solution)/shard_map/ppermute | solution.py:191
  61.7 119.3 %collective-permute-start.7 = (bf16[2,320,3584]{2,1,0:T(8,128)(2,1)S(1)}, bf16[2,320,3584]{2,1,0:T(8,128)(2,1)}, u32[]{:S(2)}, u32[]{:S(2)}) collective-permute-start(bf16[2,320,3584]{2,1,0:T(8,128)(2,1)S(1)} %constant_dynamic-update-slice_fusion.near_ref.refs_0_.refs_6_), channel_id=1, source_target_pairs={{0,8},{8,0},{16,24},{24,16},{1,9},{9,1},{17,25},{25,17},{2,10},{10... | collective-permute-start | bytes 13762568 | tf_op jit(solution)/shard_map/ppermute | solution.py:194
  61.8 66.0 %collective-permute-start.13 = (bf16[80,3584]{1,0:T(8,128)(2,1)S(1)}, bf16[80,3584]{1,0:T(8,128)(2,1)S(1)}, u32[]{:S(2)}, u32[]{:S(2)}) collective-permute-start(bf16[80,3584]{1,0:T(8,128)(2,1)S(1)} %copy-done.15), channel_id=1, source_target_pairs={{0,4},{1,5},{2,6},{3,7},{4,0},{5,1},{6,2},{7,3},{8,12},{9,13},{10,... | collective-permute-start | bytes 1720328 | tf_op jit(solution)/shard_map/ppermute | solution.py:188
  64.4 76.6 %collective-permute-start.14 = (bf16[80,3584]{1,0:T(8,128)(2,1)S(1)}, bf16[80,3584]{1,0:T(8,128)(2,1)S(1)}, u32[]{:S(2)}, u32[]{:S(2)}) collective-permute-start(bf16[80,3584]{1,0:T(8,128)(2,1)S(1)} %copy-done.14), channel_id=1, source_target_pairs={{0,5},{1,4},{2,7},{3,6},{4,1},{5,0},{6,3},{7,2},{8,13},{9,12},{10,... | collective-permute-start | bytes 1720328 | tf_op jit(solution)/shard_map/ppermute | solution.py:188
  65.7 76.8 %collective-permute-start.22 = (bf16[80,3584]{1,0:T(8,128)(2,1)S(1)}, bf16[80,3584]{1,0:T(8,128)(2,1)S(1)}, u32[]{:S(2)}, u32[]{:S(2)}) collective-permute-start(bf16[80,3584]{1,0:T(8,128)(2,1)S(1)} %copy-done.13), channel_id=1, source_target_pairs={{0,6},{1,7},{2,4},{3,5},{4,2},{5,3},{6,0},{7,1},{8,14},{9,15},{10,... | collective-permute-start | bytes 1720328 | tf_op jit(solution)/shard_map/ppermute | solution.py:188
  69.3 73.7 %collective-permute-start.23 = (bf16[80,3584]{1,0:T(8,128)(2,1)S(1)}, bf16[80,3584]{1,0:T(8,128)(2,1)S(1)}, u32[]{:S(2)}, u32[]{:S(2)}) collective-permute-start(bf16[80,3584]{1,0:T(8,128)(2,1)S(1)} %copy-done.12), channel_id=1, source_target_pairs={{0,7},{1,6},{2,5},{3,4},{4,3},{5,2},{6,1},{7,0},{8,15},{9,14},{10,... | collective-permute-start | bytes 1720328 | tf_op jit(solution)/shard_map/ppermute | solution.py:188
  127.8 16.7 %collective-permute-start.15 = (bf16[80,3584]{1,0:T(8,128)(2,1)S(1)}, bf16[80,3584]{1,0:T(8,128)(2,1)S(1)}, u32[]{:S(2)}, u32[]{:S(2)}) collective-permute-start(bf16[80,3584]{1,0:T(8,128)(2,1)S(1)} %collective-permute-done.13), channel_id=1, source_target_pairs={{0,16},{8,24},{16,0},{24,8},{1,17},{9,25},{17,1},{25,9},{2,18},{10... | collective-permute-start | bytes 1720328 | tf_op jit(solution)/shard_map/ppermute | solution.py:191
  140.9 15.8 %collective-permute-start.16 = (bf16[80,3584]{1,0:T(8,128)(2,1)S(1)}, bf16[80,3584]{1,0:T(8,128)(2,1)S(1)}, u32[]{:S(2)}, u32[]{:S(2)}) collective-permute-start(bf16[80,3584]{1,0:T(8,128)(2,1)S(1)} %collective-permute-done.14), channel_id=1, source_target_pairs={{0,16},{8,24},{16,0},{24,8},{1,17},{9,25},{17,1},{25,9},{2,18},{10... | collective-permute-start | bytes 1720328 | tf_op jit(solution)/shard_map/ppermute | solution.py:191
  142.4 26.6 %collective-permute-start.24 = (bf16[80,3584]{1,0:T(8,128)(2,1)S(1)}, bf16[80,3584]{1,0:T(8,128)(2,1)S(1)}, u32[]{:S(2)}, u32[]{:S(2)}) collective-permute-start(bf16[80,3584]{1,0:T(8,128)(2,1)S(1)} %collective-permute-done.22), channel_id=1, source_target_pairs={{0,16},{8,24},{16,0},{24,8},{1,17},{9,25},{17,1},{25,9},{2,18},{10... | collective-permute-start | bytes 1720328 | tf_op jit(solution)/shard_map/ppermute | solution.py:191
  142.9 36.4 %collective-permute-start.25 = (bf16[80,3584]{1,0:T(8,128)(2,1)S(1)}, bf16[80,3584]{1,0:T(8,128)(2,1)S(1)}, u32[]{:S(2)}, u32[]{:S(2)}) collective-permute-start(bf16[80,3584]{1,0:T(8,128)(2,1)S(1)} %collective-permute-done.23), channel_id=1, source_target_pairs={{0,16},{8,24},{16,0},{24,8},{1,17},{9,25},{17,1},{25,9},{2,18},{10... | collective-permute-start | bytes 1720328 | tf_op jit(solution)/shard_map/ppermute | solution.py:191
  156.9 43.2 %collective-permute-start.17 = (bf16[2,160,3584]{2,1,0:T(8,128)(2,1)S(1)}, bf16[2,160,3584]{2,1,0:T(8,128)(2,1)}, u32[]{:S(2)}, u32[]{:S(2)}) collective-permute-start(bf16[2,160,3584]{2,1,0:T(8,128)(2,1)S(1)} %pad_maximum_fusion.near_ref.refs_1_.refs_7_), channel_id=1, source_target_pairs={{0,8},{8,0},{16,24},{24,16},{1,9},{9,1},{17,25},{25,17},{2,10},{10... | collective-permute-start | bytes 6881288 | tf_op jit(solution)/shard_map/ppermute | solution.py:194
  181.0 31.9 %collective-permute-start.26 = (bf16[2,160,3584]{2,1,0:T(8,128)(2,1)}, bf16[2,160,3584]{2,1,0:T(8,128)(2,1)}, u32[]{:S(2)}, u32[]{:S(2)}) collective-permute-start(bf16[2,160,3584]{2,1,0:T(8,128)(2,1)} %pad_maximum_fusion.1.near_ref.refs_2_.refs_8_), channel_id=1, source_target_pairs={{0,8},{8,0},{16,24},{24,16},{1,9},{9,1},{17,25},{25,17},{2,10},{10... | collective-permute-start | bytes 6881288 | tf_op jit(solution)/shard_map/ppermute | solution.py:194
  199.5 28.4 %collective-permute-start.8 = (bf16[2,320,1920]{2,1,0:T(8,128)(2,1)}, bf16[2,320,1920]{2,1,0:T(8,128)(2,1)}, u32[]{:S(2)}, u32[]{:S(2)}) collective-permute-start(bf16[2,320,1920]{2,1,0:T(8,128)(2,1)} %get-tuple-element.47), channel_id=1, source_target_pairs={{0,8},{8,0},{16,24},{24,16},{1,9},{9,1},{17,25},{25,17},{2,10},{10... | collective-permute-start | bytes 7372808 | tf_op jit(solution)/shard_map/ppermute | solution.py:194
  212.7 13.5 %collective-permute-start.18 = (bf16[2,160,1920]{2,1,0:T(8,128)(2,1)}, bf16[2,160,1920]{2,1,0:T(8,128)(2,1)S(1)}, u32[]{:S(2)}, u32[]{:S(2)}) collective-permute-start(bf16[2,160,1920]{2,1,0:T(8,128)(2,1)} %get-tuple-element.51), channel_id=1, source_target_pairs={{0,8},{8,0},{16,24},{24,16},{1,9},{9,1},{17,25},{25,17},{2,10},{10... | collective-permute-start | bytes 3686408 | tf_op jit(solution)/shard_map/ppermute | solution.py:194
  225.6 4.4 %collective-permute-start.27 = (bf16[2,160,1920]{2,1,0:T(8,128)(2,1)}, bf16[2,160,1920]{2,1,0:T(8,128)(2,1)S(1)}, u32[]{:S(2)}, u32[]{:S(2)}) collective-permute-start(bf16[2,160,1920]{2,1,0:T(8,128)(2,1)} %get-tuple-element.55), channel_id=1, source_target_pairs={{0,8},{8,0},{16,24},{24,16},{1,9},{9,1},{17,25},{25,17},{2,10},{10... | collective-permute-start | bytes 3686408 | tf_op jit(solution)/shard_map/ppermute | solution.py:194
  226.3 16.8 %collective-permute-start.19 = (bf16[2,80,1920]{2,1,0:T(8,128)(2,1)S(1)}, bf16[2,80,1920]{2,1,0:T(8,128)(2,1)S(1)}, u32[]{:S(2)}, u32[]{:S(2)}) collective-permute-start(bf16[2,80,1920]{2,1,0:T(8,128)(2,1)S(1)} %add_convert_fusion.2), channel_id=1, source_target_pairs={{0,16},{8,24},{16,0},{24,8},{1,17},{9,25},{17,1},{25,9},{2,18},{10... | collective-permute-start | bytes 1843208 | tf_op jit(solution)/shard_map/ppermute | solution.py:191
  229.5 56.6 %collective-permute-start.9 = (bf16[2,160,1920]{2,1,0:T(8,128)(2,1)S(1)}, bf16[2,160,1920]{2,1,0:T(8,128)(2,1)S(1)}, u32[]{:S(2)}, u32[]{:S(2)}) collective-permute-start(bf16[2,160,1920]{2,1,0:T(8,128)(2,1)S(1)} %add_convert_fusion), channel_id=1, source_target_pairs={{0,16},{8,24},{16,0},{24,8},{1,17},{9,25},{17,1},{25,9},{2,18},{10... | collective-permute-start | bytes 3686408 | tf_op jit(solution)/shard_map/ppermute | solution.py:191
  230.2 51.5 %collective-permute-start.28 = (bf16[2,80,1920]{2,1,0:T(8,128)(2,1)S(1)}, bf16[2,80,1920]{2,1,0:T(8,128)(2,1)S(1)}, u32[]{:S(2)}, u32[]{:S(2)}) collective-permute-start(bf16[2,80,1920]{2,1,0:T(8,128)(2,1)S(1)} %add_convert_fusion.1), channel_id=1, source_target_pairs={{0,16},{8,24},{16,0},{24,8},{1,17},{9,25},{17,1},{25,9},{2,18},{10... | collective-permute-start | bytes 1843208 | tf_op jit(solution)/shard_map/ppermute | solution.py:191
  243.3 45.2 %collective-permute-start.20 = (bf16[80,1920]{1,0:T(8,128)(2,1)S(1)}, bf16[80,1920]{1,0:T(8,128)(2,1)S(1)}, u32[]{:S(2)}, u32[]{:S(2)}) collective-permute-start(bf16[80,1920]{1,0:T(8,128)(2,1)S(1)} %bitcast.53), channel_id=1, source_target_pairs={{0,4},{1,5},{2,6},{3,7},{4,0},{5,1},{6,2},{7,3},{8,12},{9,13},{10,... | collective-permute-start | bytes 921608 | tf_op jit(solution)/shard_map/ppermute | solution.py:188
  246.5 44.9 %collective-permute-start.21 = (bf16[80,1920]{1,0:T(8,128)(2,1)S(1)}, bf16[80,1920]{1,0:T(8,128)(2,1)S(1)}, u32[]{:S(2)}, u32[]{:S(2)}) collective-permute-start(bf16[80,1920]{1,0:T(8,128)(2,1)S(1)} %bitcast.52), channel_id=1, source_target_pairs={{0,5},{1,4},{2,7},{3,6},{4,1},{5,0},{6,3},{7,2},{8,13},{9,12},{10,... | collective-permute-start | bytes 921608 | tf_op jit(solution)/shard_map/ppermute | solution.py:188
  281.9 12.3 %collective-permute-start.29 = (bf16[80,1920]{1,0:T(8,128)(2,1)S(1)}, bf16[80,1920]{1,0:T(8,128)(2,1)S(1)}, u32[]{:S(2)}, u32[]{:S(2)}) collective-permute-start(bf16[80,1920]{1,0:T(8,128)(2,1)S(1)} %bitcast.55), channel_id=1, source_target_pairs={{0,6},{1,7},{2,4},{3,5},{4,2},{5,3},{6,0},{7,1},{8,14},{9,15},{10,... | collective-permute-start | bytes 921608 | tf_op jit(solution)/shard_map/ppermute | solution.py:188
  286.0 14.8 %collective-permute-start.30 = (bf16[80,1920]{1,0:T(8,128)(2,1)S(1)}, bf16[80,1920]{1,0:T(8,128)(2,1)S(1)}, u32[]{:S(2)}, u32[]{:S(2)}) collective-permute-start(bf16[80,1920]{1,0:T(8,128)(2,1)S(1)} %bitcast.54), channel_id=1, source_target_pairs={{0,7},{1,6},{2,5},{3,4},{4,3},{5,2},{6,1},{7,0},{8,15},{9,14},{10,... | collective-permute-start | bytes 921608 | tf_op jit(solution)/shard_map/ppermute | solution.py:188
  288.5 18.4 %collective-permute-start.11 = (bf16[80,1920]{1,0:T(8,128)(2,1)S(1)}, bf16[80,1920]{1,0:T(8,128)(2,1)S(1)}, u32[]{:S(2)}, u32[]{:S(2)}) collective-permute-start(bf16[80,1920]{1,0:T(8,128)(2,1)S(1)} %bitcast.51), channel_id=1, source_target_pairs={{0,2},{1,3},{2,0},{3,1},{4,6},{5,7},{6,4},{7,5},{8,10},{9,11},{10,... | collective-permute-start | bytes 921608 | tf_op jit(solution)/shard_map/ppermute | solution.py:188
  288.5 27.3 %collective-permute-start.12 = (bf16[80,1920]{1,0:T(8,128)(2,1)S(1)}, bf16[80,1920]{1,0:T(8,128)(2,1)S(1)}, u32[]{:S(2)}, u32[]{:S(2)}) collective-permute-start(bf16[80,1920]{1,0:T(8,128)(2,1)S(1)} %bitcast.50), channel_id=1, source_target_pairs={{0,3},{1,2},{2,1},{3,0},{4,7},{5,6},{6,5},{7,4},{8,11},{9,10},{10,... | collective-permute-start | bytes 921608 | tf_op jit(solution)/shard_map/ppermute | solution.py:188
  291.4 24.4 %collective-permute-start.10 = (bf16[80,1920]{1,0:T(8,128)(2,1)S(1)}, bf16[80,1920]{1,0:T(8,128)(2,1)S(1)}, u32[]{:S(2)}, u32[]{:S(2)}) collective-permute-start(bf16[80,1920]{1,0:T(8,128)(2,1)S(1)} %bitcast.49), channel_id=1, source_target_pairs={{0,1},{1,0},{2,3},{3,2},{4,5},{5,4},{6,7},{7,6},{8,9},{9,8},{10,11... | collective-permute-start | bytes 921608 | tf_op jit(solution)/shard_map/ppermute | solution.py:188
  321.4 32.1 %all-to-all-start = ((f32[32,24,128]{2,1,0:T(8,128)}), f32[32,24,128]{2,1,0:T(8,128)S(1)}, u32[]{:S(2)}, u32[]{:S(2)}) async-start(f32[32,24,128]{2,1,0:T(8,128)} %get-tuple-element.77), calls=%async_computation | async-start | bytes 786432 | tf_op jit(solution)/shard_map/all_to_all | solution.py:287
  (16 other events, 412.5 us)
where the time goes:
time: 355 us
  waiting for transfers between devices  219 us (62%)
  Pallas kernels  80.3 us (23%)
  starting transfers between devices  43.5 us (12%)
  other arithmetic  6.5 us (2%)
  local copies, waits for them, and re-layouts  4.06 us (1%)
    ppermute x14, waiting for transfers between devices, across(): return lax.ppermute(value, 'ctx', [(i, i ^ s) for i in range(n_ctx)])  114 us
    ppermute x11, waiting for transfers between devices, chip(): return lax.ppermute(value, 'dp', [(i, i ^ 2) for i in range(n_dp)])  105 us
    pallas_call x3, Pallas kernels, expert_pass(): pl.pallas_call(functools.partial(expert_kernel, width), grid=(local,), in...  44 us
    pallas_call x2, Pallas kernels, weights(): pl.pallas_call(functools.partial(weight_kernel, count), grid=(local,), in...  27.3 us
    ppermute x14, starting transfers between devices, across(): return lax.ppermute(value, 'ctx', [(i, i ^ s) for i in range(n_ctx)])  23.1 us
    ppermute x11, starting transfers between devices, chip(): return lax.ppermute(value, 'dp', [(i, i ^ 2) for i in range(n_dp)])  14.2 us
  transfers between devices with their start and end apart: 32, of which 16 were waited for; matrix products, arithmetic and copies ran while one was open for 2% of the time, Pallas kernels for 20%

commit v1 on v0

--- a/solution.py
+++ b/solution.py
@@ -159,6 +159,34 @@
     ).astype(BF)
 
 
+def add_kernel(*refs):
+    total = refs[0][...].astype(F32)
+    for ref in refs[1:-1]:
+        total = total + ref[...].astype(F32)
+    refs[-1][...] = total.astype(BF)
+
+
+def add_pieces(*terms, count):
+    local, _, cap, wide = terms[0][0].shape
+    block = (local, 1, cap, wide)
+    return pl.pallas_call(
+        add_kernel,
+        grid=(count,),
+        in_specs=[pl.BlockSpec(block, lambda i, at=at: (0, at + i, 0, 0)) for _, at in terms],
+        out_specs=pl.BlockSpec(block, lambda i: (0, i, 0, 0)),
+        out_shape=jax.ShapeDtypeStruct((local, count, cap, wide), BF),
+        name="add",
+    )(*[value for value, _ in terms])
+
+
+def plan(n_ctx):
+    if n_ctx == 8:
+        return ((0, 1, 2, 4), (3, 5), (6, 7)), (((4,), (0,), (1, 2)), ((5,), (3,)), ((6,), (7,)))
+    half, quarter = n_ctx // 2, n_ctx // 4
+    groups = (tuple(range(half)), tuple(range(half, half + quarter)), tuple(range(half + quarter, n_ctx)))
+    return groups, tuple((g,) for g in groups)
+
+
 def body(tokens, cotangent, expert_ids, norm_gain, router_weight, gate_weight, up_weight, down_weight):
     n_ctx, n_dp = lax.axis_size("ctx"), lax.axis_size("dp")
     me = lax.axis_index("ctx")
@@ -193,8 +221,7 @@
     def core(value):
         return lax.ppermute(value, "dp", [(i, i ^ 1) for i in range(n_dp)])
 
-    half, quarter = n_ctx // 2, n_ctx // 4
-    groups = (range(half), range(half, half + quarter), range(half + quarter, n_ctx))
+    groups, units = plan(n_ctx)
     arrived = {s: across(messages[s], s) if s else messages[s] for s in range(n_ctx)}
     crossed = {s: chip(arrived[s]) for s in range(n_ctx)}
 
@@ -216,24 +243,23 @@
 
     done = []
     for group in groups:
-        parts = [arrived[s] for s in group] + [crossed[s] for s in group]
+        parts = lax.optimization_barrier([arrived[s] for s in group] + [crossed[s] for s in group])
         near = jnp.concatenate([p.reshape(local, cap, 2 * width) for p in parts], axis=1)
         far = core(near)
         done.append((near, far, *expert_pass(near, far)))
 
     returned = {}
-    for g in (1, 2, 0):
-        group = groups[g]
-        size = len(group) * cap
-        back_near, back_far = done[g][2], done[g][5]
-        other = core(back_far)
-        leave = (back_near[:, size:].astype(F32) + other[:, size:].astype(F32)).astype(BF)
-        came = chip(leave)
-        for i, s in enumerate(group):
-            cut = slice(i * cap, (i + 1) * cap)
-            final = back_near[:, cut].astype(F32) + other[:, cut].astype(F32) + came[:, cut].astype(F32)
-            final = final.astype(BF).reshape(slots, wide)
-            returned[s] = across(final, s) if s else final
+    for g, group in enumerate(groups):
+        split = lambda v: v.reshape(local, 2 * len(group), cap, wide)
+        near, other = split(done[g][2]), split(core(done[g][5]))
+        for unit in units[g]:
+            first, size = group.index(unit[0]), len(unit)
+            leave = add_pieces((near, len(group) + first), (other, len(group) + first), count=size)
+            came = chip(leave)
+            for i, s in enumerate(unit):
+                final = add_pieces((near, first + i), (other, first + i), (came, i), count=1)
+                final = final.reshape(slots, wide)
+                returned[s] = across(final, s) if s else final
 
     near_rows = [d[0] for d in done] + [d[1] for d in done]
     hiddens = [d[3] for d in done] + [d[6] for d in done]
@@ -274,10 +300,7 @@
     lines = -(-(experts + 1) // 8) * 8
     grad_input, part = pl.pallas_call(
         functools.partial(tail_kernel, local, cap, experts, shard, n_ctx),
-        out_shape=[
-            jax.ShapeDtypeStruct((rows_here, width), BF),
-            jax.ShapeDtypeStruct((devices, lines, LANES), F32),
-        ],
+        out_shape=[jax.ShapeDtypeStruct((rows_here, width), BF), jax.ShapeDtypeStruct((devices, lines, LANES), F32)],
         in_specs=vmem(n_ctx + 7),
         out_specs=vmem(2),
         scratch_shapes=[pltpu.VMEM((LANES, rows_here), F32)],

time: 355 us -> 341 us (0.961)
  waiting for transfers between devices: 219 us -> 164 us
  Pallas kernels: 80.3 us -> 109 us
  starting transfers between devices: 43.5 us -> 56.1 us
    ppermute x14, waiting for transfers between devices: 114 us -> 85 us  [across(): return lax.ppermute(value, 'ctx', [(i, i ^ s) for i in range(n_ctx)])]
    pallas_call x0 -> x15, Pallas kernels: none -> 29.2 us  [add_pieces(): pl.pallas_call(add_kernel, grid=(count,), in_specs=[pl.BlockSpec(block, l...]
    ppermute x11 -> x15, waiting for transfers between devices: 105 us -> 79.1 us  [chip(): return lax.ppermute(value, 'dp', [(i, i ^ 2) for i in range(n_dp)])]
    ppermute x14, starting transfers between devices: 23.1 us -> 33.4 us  [across(): return lax.ppermute(value, 'ctx', [(i, i ^ s) for i in range(n_ctx)])]
    convert_element_type x6 -> x0, other arithmetic: 4.75 us -> none  [the longest x3 2.89 us: body(): final = final.astype(BF).reshape(slots, wide)]
    ppermute x11 -> x15, starting transfers between devices: 14.2 us -> 18.8 us  [chip(): return lax.ppermute(value, 'dp', [(i, i ^ 2) for i in range(n_dp)])]
  transfers between devices with their start and end apart: 32 -> 36, of which waited for: 16 -> 15; matrix products, arithmetic and copies ran while one was open for 2% -> 1% of each run, Pallas kernels for 20% -> 29%
where the time goes in v1:
time: 341 us; the launch traced here: 340 us
  waiting for transfers between devices  164 us (48%)
  Pallas kernels  109 us (32%)
  starting transfers between devices  56.1 us (16%)
  local copies, waits for them, and re-layouts  6.63 us (2%)
    ppermute x14, waiting for transfers between devices, across(): return lax.ppermute(value, 'ctx', [(i, i ^ s) for i in range(n_ctx)])  85 us
    ppermute x15, waiting for transfers between devices, chip(): return lax.ppermute(value, 'dp', [(i, i ^ 2) for i in range(n_dp)])  79.1 us
    pallas_call x3, Pallas kernels, expert_pass(): pl.pallas_call(functools.partial(expert_kernel, width), grid=(local,), in...  43.8 us
    ppermute x14, starting transfers between devices, across(): return lax.ppermute(value, 'ctx', [(i, i ^ s) for i in range(n_ctx)])  33.4 us
    pallas_call x15, Pallas kernels, add_pieces(): pl.pallas_call(add_kernel, grid=(count,), in_specs=[pl.BlockSpec(block, l...  29.2 us
    pallas_call x2, Pallas kernels, weights(): pl.pallas_call(functools.partial(weight_kernel, count), grid=(local,), in...  27.3 us
    ppermute x15, starting transfers between devices, chip(): return lax.ppermute(value, 'dp', [(i, i ^ 2) for i in range(n_dp)])  18.8 us
  transfers between devices with their start and end apart: 36, of which 15 were waited for; matrix products, arithmetic and copies ran while one was open for 1% of the time, Pallas kernels for 29%

profile of v1, /device:TPU:0, one launch (start us, length us, event | category | flops | bytes accessed | tf_op | source)
XLA Modules:
  0.0 340.2 jit_solution(13441342141634357833)
XLA Ops:
  1.4 4.3 %head.1 = (bf16[80,3584]{1,0:T(8,128)(2,1)}, bf16[80,3584]{1,0:T(8,128)(2,1)}, bf16[80,3584]{1,0:T(8,128)(2,1)}, bf16[80,3584]{1,0:T(8,128)(2,1)}, bf16[80,3584]...) custom-call(bf16[128,1792]{1,0:T(8,128)(2,1)} %refs_10_.1, ...), custom_call_target="tpu_custom_call" | custom-call | tf_op jit(solution)/shard_map/head/pallas_call | solution.py:205
  5.6 3.0 collective-permute-start
  10.2 2.6 collective-permute-start.2
  14.3 7.5 %collective-permute-done = bf16[80,3584]{1,0:T(8,128)(2,1)S(1)} collective-permute-done((bf16[80,3584]{1,0:T(8,128)(2,1)}, bf16[80,3584]{1,0:T(8,128)(2,1)S(1)}, u32[]{:S(2)}, u32[]{:S(2)}) %collective-permute-start) | collective-permute-done | bytes 573472 | tf_op jit(solution)/shard_map/ppermute | solution.py:216
  23.5 11.9 %collective-permute-done.1 = bf16[80,3584]{1,0:T(8,128)(2,1)S(1)} collective-permute-done((bf16[80,3584]{1,0:T(8,128)(2,1)}, bf16[80,3584]{1,0:T(8,128)(2,1)S(1)}, u32[]{:S(2)}, u32[]{:S(2)}) %collective-permute-start.1) | collective-permute-done | bytes 573472 | tf_op jit(solution)/shard_map/ppermute | solution.py:216
  41.2 12.3 %collective-permute-done.5 = bf16[80,3584]{1,0:T(8,128)(2,1)S(1)} collective-permute-done((bf16[80,3584]{1,0:T(8,128)(2,1)S(1)}, bf16[80,3584]{1,0:T(8,128)(2,1)S(1)}, u32[]{:S(2)}, u32[]{:S(2)}) %collective-permute-start.5) | collective-permute-done | bytes 573472 | tf_op jit(solution)/shard_map/ppermute | solution.py:219
  53.5 10.3 %collective-permute-done.6 = bf16[80,3584]{1,0:T(8,128)(2,1)S(1)} collective-permute-done((bf16[80,3584]{1,0:T(8,128)(2,1)S(1)}, bf16[80,3584]{1,0:T(8,128)(2,1)S(1)}, u32[]{:S(2)}, u32[]{:S(2)}) %collective-permute-start.6) | collective-permute-done | bytes 573472 | tf_op jit(solution)/shard_map/ppermute | solution.py:219
  67.3 3.5 %collective-permute-start.25 = (bf16[80,3584]{1,0:T(8,128)(2,1)S(1)}, bf16[80,3584]{1,0:T(8,128)(2,1)S(1)}, u32[]{:S(2)}, u32[]{:S(2)}) collective-permute-start(bf16[80,3584]{1,0:T(8,128)(2,1)S(1)} %copy-done.20), channel_id=1, source_target_pairs={{0,6},{1,7},{2,4},{3,5},{4,2},{5,3},{6,0},{7,1},{8,14},{9,15},{10,... | collective-permute-start | bytes 1720328 | tf_op jit(solution)/shard_map/ppermute | solution.py:216
  72.1 20.7 %collective-permute-done.13 = bf16[80,3584]{1,0:T(8,128)(2,1)S(1)} collective-permute-done((bf16[80,3584]{1,0:T(8,128)(2,1)S(1)}, bf16[80,3584]{1,0:T(8,128)(2,1)S(1)}, u32[]{:S(2)}, u32[]{:S(2)}) %collective-permute-start.13) | collective-permute-done | bytes 573472 | tf_op jit(solution)/shard_map/ppermute | solution.py:216
  94.3 26.2 %collective-permute-done.14 = bf16[80,3584]{1,0:T(8,128)(2,1)S(1)} collective-permute-done((bf16[80,3584]{1,0:T(8,128)(2,1)S(1)}, bf16[80,3584]{1,0:T(8,128)(2,1)S(1)}, u32[]{:S(2)}, u32[]{:S(2)}) %collective-permute-start.14) | collective-permute-done | bytes 573472 | tf_op jit(solution)/shard_map/ppermute | solution.py:216
  124.0 12.3 %collective-permute-done.16 = bf16[80,3584]{1,0:T(8,128)(2,1)S(1)} collective-permute-done((bf16[80,3584]{1,0:T(8,128)(2,1)S(1)}, bf16[80,3584]{1,0:T(8,128)(2,1)S(1)}, u32[]{:S(2)}, u32[]{:S(2)}) %collective-permute-start.16) | collective-permute-done | bytes 573472 | tf_op jit(solution)/shard_map/ppermute | solution.py:219
  136.3 12.3 %collective-permute-done.27 = bf16[80,3584]{1,0:T(8,128)(2,1)S(1)} collective-permute-done((bf16[80,3584]{1,0:T(8,128)(2,1)S(1)}, bf16[80,3584]{1,0:T(8,128)(2,1)S(1)}, u32[]{:S(2)}, u32[]{:S(2)}) %collective-permute-start.27) | collective-permute-done | bytes 573472 | tf_op jit(solution)/shard_map/ppermute | solution.py:219
  148.6 9.8 %collective-permute-done.28 = bf16[80,3584]{1,0:T(8,128)(2,1)S(1)} collective-permute-done((bf16[80,3584]{1,0:T(8,128)(2,1)S(1)}, bf16[80,3584]{1,0:T(8,128)(2,1)S(1)}, u32[]{:S(2)}, u32[]{:S(2)}) %collective-permute-start.28) | collective-permute-done | bytes 573472 | tf_op jit(solution)/shard_map/ppermute | solution.py:219
  161.9 18.5 %expert.3 = (bf16[2,320,1920]{2,1,0:T(8,128)(2,1)}, bf16[2,320,384]{2,1,0:T(8,128)(2,1)}, bf16[2,320,768]{2,1,0:T(8,128)(2,1)}, bf16[2,320,1920]{2,1,0:T(8,128)(...) custom-call(bf16[2,320,3584]{2,1,0:T(8,128)(2,1)} %copy-done.1, ...), custom_call_target="tpu_custom_call" | custom-call | flops 8808038400 | bytes 9175040 | tf_op jit(solution)/shard_map/expert/pallas_call | solution.py:233
  180.5 12.6 %expert.4 = (bf16[2,160,1920]{2,1,0:T(8,128)(2,1)}, bf16[2,160,384]{2,1,0:T(8,128)(2,1)}, bf16[2,160,768]{2,1,0:T(8,128)(2,1)}, bf16[2,160,1920]{2,1,0:T(8,128)(...) custom-call(bf16[2,160,3584]{2,1,0:T(8,128)(2,1)} %pad_maximum_fusion.near_ref.refs_1_.refs_7_, ...), custom_call_target="tpu_custom_call" | custom-call | flops 4404019200 | bytes 4587520 | tf_op jit(solution)/shard_map/expert/pallas_call | solution.py:233
  193.7 12.7 %expert.5 = (bf16[2,160,1920]{2,1,0:T(8,128)(2,1)}, bf16[2,160,384]{2,1,0:T(8,128)(2,1)}, bf16[2,160,768]{2,1,0:T(8,128)(2,1)}, bf16[2,160,1920]{2,1,0:T(8,128)(...) custom-call(bf16[2,160,3584]{2,1,0:T(8,128)(2,1)} %pad_maximum_fusion.1.near_ref.refs_2_.refs_8_, ...), custom_call_target="tpu_custom_call" | custom-call | flops 4404019200 | bytes 4587520 | tf_op jit(solution)/shard_map/expert/pallas_call | solution.py:233
  213.7 2.0 add.35
  225.6 2.0 add.39
  229.1 2.0 add.43
  231.1 15.8 %collective-permute-done.31.refs_2_ = bf16[2,1,40,1920]{3,2,1,0:T(8,128)(2,1)S(1)} collective-permute-done((bf16[2,1,40,1920]{3,2,1,0:T(8,128)(2,1)}, bf16[2,1,40,1920]{3,2,1,0:T(8,128)(2,1)S(1)}, u32[]{:S(2)}, u32[]{:S(2)}) %collective-permute-start.31) | collective-permute-done | bytes 307232 | tf_op jit(solution)/shard_map/ppermute | solution.py:219
  250.1 3.3 collective-permute-done.33.refs_2_
  256.9 2.0 add.47
  260.8 2.0 add.41
  262.8 4.1 %collective-permute-start.34 = (bf16[80,1920]{1,0:T(8,128)(2,1)S(1)}, bf16[80,1920]{1,0:T(8,128)(2,1)S(1)}, u32[]{:S(2)}, u32[]{:S(2)}) collective-permute-start(bf16[80,1920]{1,0:T(8,128)(2,1)S(1)} %bitcast.80), channel_id=1, source_target_pairs={{0,7},{1,6},{2,5},{3,4},{4,3},{5,2},{6,1},{7,0},{8,15},{9,14},{10,... | collective-permute-start | bytes 921608 | tf_op jit(solution)/shard_map/ppermute | solution.py:216
  266.9 2.0 add.37
  268.9 2.1 add.36
  271.1 11.2 %collective-permute-start.12 = (bf16[80,1920]{1,0:T(8,128)(2,1)S(1)}, bf16[80,1920]{1,0:T(8,128)(2,1)S(1)}, u32[]{:S(2)}, u32[]{:S(2)}) collective-permute-start(bf16[80,1920]{1,0:T(8,128)(2,1)S(1)} %bitcast.78), channel_id=1, source_target_pairs={{0,2},{1,3},{2,0},{3,1},{4,6},{5,7},{6,4},{7,5},{8,10},{9,11},{10,... | collective-permute-start | bytes 921608 | tf_op jit(solution)/shard_map/ppermute | solution.py:216
  285.6 17.8 %collective-permute-done.22.refs_4_ = bf16[80,1920]{1,0:T(8,128)(2,1)S(1)} collective-permute-done((bf16[80,1920]{1,0:T(8,128)(2,1)S(1)}, bf16[80,1920]{1,0:T(8,128)(2,1)S(1)}, u32[]{:S(2)}, u32[]{:S(2)}) %collective-permute-start.22) | collective-permute-done | bytes 307232 | tf_op jit(solution)/shard_map/ppermute | solution.py:216
  304.3 4.8 %tail.1 = (bf16[128,1792]{1,0:T(8,128)(2,1)}, f32[32,24,128]{2,1,0:T(8,128)}) custom-call(bf16[80,1920]{1,0:T(8,128)(2,1)} %bitcast.60, bf16[80,1920]{1,0:T(8,128)(2,1)} %copy-done.15, bf16[80,1920]{1,0:T(8,128)(2,1)} %copy-done.13, bf16[80,1920]{1,0:T(8,128)(2,1)} %copy-done.4, bf16[80,1920]{1,0:T(8,128)(2,1)} %copy-done.9, bf16[80,1920]{1,0:T(8,128)(2,1)} %copy-done.5, ...), custom_call_target="tpu_custom_call" | custom-call | tf_op jit(solution)/shard_map/tail/pallas_call | solution.py:301
  309.1 2.6 all-to-all-start
  311.7 13.6 %shard_map.127 = (bf16[2,1792,384]{2,1,0:T(8,128)(2,1)}, bf16[2,1792,384]{2,1,0:T(8,128)(2,1)}, bf16[2,384,1792]{2,1,0:T(8,128)(2,1)}) custom-call(bf16[2,320,3584]{2,1,0:T(8,128)(2,1)} %copy-done.1, bf16[2,160,3584]{2,1,0:T(8,128)(2,1)} %pad_maximum_fusion.near_ref.refs_1_.refs_7_, bf16[2,160,3584]{2,1,0:T(8,128)(2,1)} %pad_maximum_fusion.1.near_ref.refs_2_.refs_8_, ...), custom_call_target="tpu_custom_call" | custom-call | flops 5284823040 | bytes 9175040 | tf_op jit(solution)/shard_map/pallas_call | solution.py:278
  325.3 13.7 %shard_map.128 = (bf16[2,1792,384]{2,1,0:T(8,128)(2,1)}, bf16[2,1792,384]{2,1,0:T(8,128)(2,1)}, bf16[2,384,1792]{2,1,0:T(8,128)(2,1)}) custom-call(bf16[2,320,3584]{2,1,0:T(8,128)(2,1)} %copy-done.1, bf16[2,160,3584]{2,1,0:T(8,128)(2,1)} %pad_maximum_fusion.near_ref.refs_1_.refs_7_, ...), custom_call_target="tpu_custom_call", output_to_operand_aliasing={{0}: (24, {}), {1}: (25, {}), {2}: (26, {})} | custom-call | flops 5284823040 | bytes 9175040 | tf_op jit(solution)/shard_map/pallas_call | solution.py:278
  (124 shorter events, 57.6 us)
Async XLA Ops:
  5.6 16.2 %collective-permute-start = (bf16[80,3584]{1,0:T(8,128)(2,1)}, bf16[80,3584]{1,0:T(8,128)(2,1)S(1)}, u32[]{:S(2)}, u32[]{:S(2)}) collective-permute-start(bf16[80,3584]{1,0:T(8,128)(2,1)} %get-tuple-element.59), channel_id=1, source_target_pairs={{0,1},{1,0},{2,3},{3,2},{4,5},{5,4},{6,7},{7,6},{8,9},{9,8},{10,11... | collective-permute-start | bytes 1720328 | tf_op jit(solution)/shard_map/ppermute | solution.py:216
  8.6 26.8 %collective-permute-start.1 = (bf16[80,3584]{1,0:T(8,128)(2,1)}, bf16[80,3584]{1,0:T(8,128)(2,1)S(1)}, u32[]{:S(2)}, u32[]{:S(2)}) collective-permute-start(bf16[80,3584]{1,0:T(8,128)(2,1)} %get-tuple-element.60), channel_id=1, source_target_pairs={{0,2},{1,3},{2,0},{3,1},{4,6},{5,7},{6,4},{7,5},{8,10},{9,11},{10,... | collective-permute-start | bytes 1720328 | tf_op jit(solution)/shard_map/ppermute | solution.py:216
  10.2 27.6 %collective-permute-start.2 = (bf16[80,3584]{1,0:T(8,128)(2,1)}, bf16[80,3584]{1,0:T(8,128)(2,1)S(1)}, u32[]{:S(2)}, u32[]{:S(2)}) collective-permute-start(bf16[80,3584]{1,0:T(8,128)(2,1)} %get-tuple-element.61), channel_id=1, source_target_pairs={{0,4},{1,5},{2,6},{3,7},{4,0},{5,1},{6,2},{7,3},{8,12},{9,13},{10,... | collective-permute-start | bytes 1720328 | tf_op jit(solution)/shard_map/ppermute | solution.py:216
  12.8 26.5 %collective-permute-start.3 = (bf16[80,3584]{1,0:T(8,128)(2,1)}, bf16[80,3584]{1,0:T(8,128)(2,1)S(1)}, u32[]{:S(2)}, u32[]{:S(2)}) collective-permute-start(bf16[80,3584]{1,0:T(8,128)(2,1)} %get-tuple-element.62), channel_id=1, source_target_pairs={{0,16},{8,24},{16,0},{24,8},{1,17},{9,25},{17,1},{25,9},{2,18},{10... | collective-permute-start | bytes 1720328 | tf_op jit(solution)/shard_map/ppermute | solution.py:219
  21.8 19.3 %collective-permute-start.4 = (bf16[80,3584]{1,0:T(8,128)(2,1)S(1)}, bf16[80,3584]{1,0:T(8,128)(2,1)S(1)}, u32[]{:S(2)}, u32[]{:S(2)}) collective-permute-start(bf16[80,3584]{1,0:T(8,128)(2,1)S(1)} %collective-permute-done), channel_id=1, source_target_pairs={{0,16},{8,24},{16,0},{24,8},{1,17},{9,25},{17,1},{25,9},{2,18},{10... | collective-permute-start | bytes 1720328 | tf_op jit(solution)/shard_map/ppermute | solution.py:219
  35.5 18.0 %collective-permute-start.5 = (bf16[80,3584]{1,0:T(8,128)(2,1)S(1)}, bf16[80,3584]{1,0:T(8,128)(2,1)S(1)}, u32[]{:S(2)}, u32[]{:S(2)}) collective-permute-start(bf16[80,3584]{1,0:T(8,128)(2,1)S(1)} %collective-permute-done.1), channel_id=1, source_target_pairs={{0,16},{8,24},{16,0},{24,8},{1,17},{9,25},{17,1},{25,9},{2,18},{10... | collective-permute-start | bytes 1720328 | tf_op jit(solution)/shard_map/ppermute | solution.py:219
  37.8 25.9 %collective-permute-start.6 = (bf16[80,3584]{1,0:T(8,128)(2,1)S(1)}, bf16[80,3584]{1,0:T(8,128)(2,1)S(1)}, u32[]{:S(2)}, u32[]{:S(2)}) collective-permute-start(bf16[80,3584]{1,0:T(8,128)(2,1)S(1)} %collective-permute-done.2), channel_id=1, source_target_pairs={{0,16},{8,24},{16,0},{24,8},{1,17},{9,25},{17,1},{25,9},{2,18},{10... | collective-permute-start | bytes 1720328 | tf_op jit(solution)/shard_map/ppermute | solution.py:219
  65.4 96.6 %collective-permute-start.7 = (bf16[2,320,3584]{2,1,0:T(8,128)(2,1)S(1)}, bf16[2,320,3584]{2,1,0:T(8,128)(2,1)}, u32[]{:S(2)}, u32[]{:S(2)}) collective-permute-start(bf16[2,320,3584]{2,1,0:T(8,128)(2,1)S(1)} %constant_dynamic-update-slice_fusion.near_ref.refs_0_.refs_6_), channel_id=1, source_target_pairs={{0,8},{8,0},{16,24},{24,16},{1,9},{9,1},{17,25},{25,17},{2,10},{10... | collective-permute-start | bytes 13762568 | tf_op jit(solution)/shard_map/ppermute | solution.py:222
  65.5 27.4 %collective-permute-start.13 = (bf16[80,3584]{1,0:T(8,128)(2,1)S(1)}, bf16[80,3584]{1,0:T(8,128)(2,1)S(1)}, u32[]{:S(2)}, u32[]{:S(2)}) collective-permute-start(bf16[80,3584]{1,0:T(8,128)(2,1)S(1)} %copy-done.22), channel_id=1, source_target_pairs={{0,3},{1,2},{2,1},{3,0},{4,7},{5,6},{6,5},{7,4},{8,11},{9,10},{10,... | collective-permute-start | bytes 1720328 | tf_op jit(solution)/shard_map/ppermute | solution.py:216
  65.9 54.6 %collective-permute-start.14 = (bf16[80,3584]{1,0:T(8,128)(2,1)S(1)}, bf16[80,3584]{1,0:T(8,128)(2,1)S(1)}, u32[]{:S(2)}, u32[]{:S(2)}) collective-permute-start(bf16[80,3584]{1,0:T(8,128)(2,1)S(1)} %copy-done.21), channel_id=1, source_target_pairs={{0,5},{1,4},{2,7},{3,6},{4,1},{5,0},{6,3},{7,2},{8,13},{9,12},{10,... | collective-permute-start | bytes 1720328 | tf_op jit(solution)/shard_map/ppermute | solution.py:216
  67.3 54.7 %collective-permute-start.25 = (bf16[80,3584]{1,0:T(8,128)(2,1)S(1)}, bf16[80,3584]{1,0:T(8,128)(2,1)S(1)}, u32[]{:S(2)}, u32[]{:S(2)}) collective-permute-start(bf16[80,3584]{1,0:T(8,128)(2,1)S(1)} %copy-done.20), channel_id=1, source_target_pairs={{0,6},{1,7},{2,4},{3,5},{4,2},{5,3},{6,0},{7,1},{8,14},{9,15},{10,... | collective-permute-start | bytes 1720328 | tf_op jit(solution)/shard_map/ppermute | solution.py:216
  70.8 51.7 %collective-permute-start.26 = (bf16[80,3584]{1,0:T(8,128)(2,1)S(1)}, bf16[80,3584]{1,0:T(8,128)(2,1)S(1)}, u32[]{:S(2)}, u32[]{:S(2)}) collective-permute-start(bf16[80,3584]{1,0:T(8,128)(2,1)S(1)} %copy-done.19), channel_id=1, source_target_pairs={{0,7},{1,6},{2,5},{3,4},{4,3},{5,2},{6,1},{7,0},{8,15},{9,14},{10,... | collective-permute-start | bytes 1720328 | tf_op jit(solution)/shard_map/ppermute | solution.py:216
  92.8 31.2 %collective-permute-start.15 = (bf16[80,3584]{1,0:T(8,128)(2,1)S(1)}, bf16[80,3584]{1,0:T(8,128)(2,1)S(1)}, u32[]{:S(2)}, u32[]{:S(2)}) collective-permute-start(bf16[80,3584]{1,0:T(8,128)(2,1)S(1)} %collective-permute-done.13), channel_id=1, source_target_pairs={{0,16},{8,24},{16,0},{24,8},{1,17},{9,25},{17,1},{25,9},{2,18},{10... | collective-permute-start | bytes 1720328 | tf_op jit(solution)/shard_map/ppermute | solution.py:219
  122.0 26.6 %collective-permute-start.27 = (bf16[80,3584]{1,0:T(8,128)(2,1)S(1)}, bf16[80,3584]{1,0:T(8,128)(2,1)S(1)}, u32[]{:S(2)}, u32[]{:S(2)}) collective-permute-start(bf16[80,3584]{1,0:T(8,128)(2,1)S(1)} %collective-permute-done.25), channel_id=1, source_target_pairs={{0,16},{8,24},{16,0},{24,8},{1,17},{9,25},{17,1},{25,9},{2,18},{10... | collective-permute-start | bytes 1720328 | tf_op jit(solution)/shard_map/ppermute | solution.py:219
  122.5 35.9 %collective-permute-start.28 = (bf16[80,3584]{1,0:T(8,128)(2,1)S(1)}, bf16[80,3584]{1,0:T(8,128)(2,1)S(1)}, u32[]{:S(2)}, u32[]{:S(2)}) collective-permute-start(bf16[80,3584]{1,0:T(8,128)(2,1)S(1)} %collective-permute-done.26), channel_id=1, source_target_pairs={{0,16},{8,24},{16,0},{24,8},{1,17},{9,25},{17,1},{25,9},{2,18},{10... | collective-permute-start | bytes 1720328 | tf_op jit(solution)/shard_map/ppermute | solution.py:219
  159.9 20.6 %collective-permute-start.17 = (bf16[2,160,3584]{2,1,0:T(8,128)(2,1)}, bf16[2,160,3584]{2,1,0:T(8,128)(2,1)}, u32[]{:S(2)}, u32[]{:S(2)}) collective-permute-start(bf16[2,160,3584]{2,1,0:T(8,128)(2,1)} %pad_maximum_fusion.near_ref.refs_1_.refs_7_), channel_id=1, source_target_pairs={{0,8},{8,0},{16,24},{24,16},{1,9},{9,1},{17,25},{25,17},{2,10},{10... | collective-permute-start | bytes 6881288 | tf_op jit(solution)/shard_map/ppermute | solution.py:222
  161.4 32.3 %collective-permute-start.29 = (bf16[2,160,3584]{2,1,0:T(8,128)(2,1)}, bf16[2,160,3584]{2,1,0:T(8,128)(2,1)}, u32[]{:S(2)}, u32[]{:S(2)}) collective-permute-start(bf16[2,160,3584]{2,1,0:T(8,128)(2,1)} %pad_maximum_fusion.1.near_ref.refs_2_.refs_8_), channel_id=1, source_target_pairs={{0,8},{8,0},{16,24},{24,16},{1,9},{9,1},{17,25},{25,17},{2,10},{10... | collective-permute-start | bytes 6881288 | tf_op jit(solution)/shard_map/ppermute | solution.py:222
  180.5 31.8 %collective-permute-start.8 = (bf16[2,320,1920]{2,1,0:T(8,128)(2,1)}, bf16[2,320,1920]{2,1,0:T(8,128)(2,1)S(1)}, u32[]{:S(2)}, u32[]{:S(2)}) collective-permute-start(bf16[2,320,1920]{2,1,0:T(8,128)(2,1)} %get-tuple-element.71), channel_id=1, source_target_pairs={{0,8},{8,0},{16,24},{24,16},{1,9},{9,1},{17,25},{25,17},{2,10},{10... | collective-permute-start | bytes 7372808 | tf_op jit(solution)/shard_map/ppermute | solution.py:222
  211.7 15.9 %collective-permute-start.23 = (bf16[2,1,40,1920]{3,2,1,0:T(8,128)(2,1)}, bf16[2,1,40,1920]{3,2,1,0:T(8,128)(2,1)S(1)}, u32[]{:S(2)}, u32[]{:S(2)}) collective-permute-start(bf16[2,1,40,1920]{3,2,1,0:T(8,128)(2,1)} %add.42), channel_id=1, source_target_pairs={{0,16},{8,24},{16,0},{24,8},{1,17},{9,25},{17,1},{25,9},{2,18},{10... | collective-permute-start | bytes 921608 | tf_op jit(solution)/shard_map/ppermute | solution.py:219
  215.7 47.0 %collective-permute-start.10 = (bf16[2,2,40,1920]{3,2,1,0:T(8,128)(2,1)}, bf16[2,2,40,1920]{3,2,1,0:T(8,128)(2,1)S(1)}, u32[]{:S(2)}, u32[]{:S(2)}) collective-permute-start(bf16[2,2,40,1920]{3,2,1,0:T(8,128)(2,1)} %add.35), channel_id=1, source_target_pairs={{0,16},{8,24},{16,0},{24,8},{1,17},{9,25},{17,1},{25,9},{2,18},{10... | collective-permute-start | bytes 1843208 | tf_op jit(solution)/shard_map/ppermute | solution.py:219
  219.1 27.8 %collective-permute-start.31 = (bf16[2,1,40,1920]{3,2,1,0:T(8,128)(2,1)}, bf16[2,1,40,1920]{3,2,1,0:T(8,128)(2,1)S(1)}, u32[]{:S(2)}, u32[]{:S(2)}) collective-permute-start(bf16[2,1,40,1920]{3,2,1,0:T(8,128)(2,1)} %add.44), channel_id=1, source_target_pairs={{0,16},{8,24},{16,0},{24,8},{1,17},{9,25},{17,1},{25,9},{2,18},{10... | collective-permute-start | bytes 921608 | tf_op jit(solution)/shard_map/ppermute | solution.py:219
  221.5 32.0 %collective-permute-start.33 = (bf16[2,1,40,1920]{3,2,1,0:T(8,128)(2,1)}, bf16[2,1,40,1920]{3,2,1,0:T(8,128)(2,1)S(1)}, u32[]{:S(2)}, u32[]{:S(2)}) collective-permute-start(bf16[2,1,40,1920]{3,2,1,0:T(8,128)(2,1)} %add.46), channel_id=1, source_target_pairs={{0,16},{8,24},{16,0},{24,8},{1,17},{9,25},{17,1},{25,9},{2,18},{10... | collective-permute-start | bytes 921608 | tf_op jit(solution)/shard_map/ppermute | solution.py:219
  224.8 35.2 %collective-permute-start.21 = (bf16[2,1,40,1920]{3,2,1,0:T(8,128)(2,1)}, bf16[2,1,40,1920]{3,2,1,0:T(8,128)(2,1)S(1)}, u32[]{:S(2)}, u32[]{:S(2)}) collective-permute-start(bf16[2,1,40,1920]{3,2,1,0:T(8,128)(2,1)} %add.40), channel_id=1, source_target_pairs={{0,16},{8,24},{16,0},{24,8},{1,17},{9,25},{17,1},{25,9},{2,18},{10... | collective-permute-start | bytes 921608 | tf_op jit(solution)/shard_map/ppermute | solution.py:219
  227.5 43.4 %collective-permute-start.20 = (bf16[80,1920]{1,0:T(8,128)(2,1)}, bf16[80,1920]{1,0:T(8,128)(2,1)S(1)}, u32[]{:S(2)}, u32[]{:S(2)}) collective-permute-start(bf16[80,1920]{1,0:T(8,128)(2,1)} %bitcast.79), channel_id=1, source_target_pairs={{0,3},{1,2},{2,1},{3,0},{4,7},{5,6},{6,5},{7,4},{8,11},{9,10},{10,... | collective-permute-start | bytes 921608 | tf_op jit(solution)/shard_map/ppermute | solution.py:216
  246.9 24.2 %collective-permute-start.24 = (bf16[80,1920]{1,0:T(8,128)(2,1)}, bf16[80,1920]{1,0:T(8,128)(2,1)S(1)}, u32[]{:S(2)}, u32[]{:S(2)}) collective-permute-start(bf16[80,1920]{1,0:T(8,128)(2,1)} %bitcast.81), channel_id=1, source_target_pairs={{0,5},{1,4},{2,7},{3,6},{4,1},{5,0},{6,3},{7,2},{8,13},{9,12},{10,... | collective-permute-start | bytes 921608 | tf_op jit(solution)/shard_map/ppermute | solution.py:216
  253.5 28.9 %collective-permute-start.9 = (bf16[2,1,40,1920]{3,2,1,0:T(8,128)(2,1)}, bf16[2,1,40,1920]{3,2,1,0:T(8,128)(2,1)S(1)}, u32[]{:S(2)}, u32[]{:S(2)}) collective-permute-start(bf16[2,1,40,1920]{3,2,1,0:T(8,128)(2,1)} %add.33), channel_id=1, source_target_pairs={{0,16},{8,24},{16,0},{24,8},{1,17},{9,25},{17,1},{25,9},{2,18},{10... | collective-permute-start | bytes 921608 | tf_op jit(solution)/shard_map/ppermute | solution.py:219
  260.1 25.5 %collective-permute-start.32 = (bf16[80,1920]{1,0:T(8,128)(2,1)}, bf16[80,1920]{1,0:T(8,128)(2,1)S(1)}, u32[]{:S(2)}, u32[]{:S(2)}) collective-permute-start(bf16[80,1920]{1,0:T(8,128)(2,1)} %bitcast.82), channel_id=1, source_target_pairs={{0,6},{1,7},{2,4},{3,5},{4,2},{5,3},{6,0},{7,1},{8,14},{9,15},{10,... | collective-permute-start | bytes 921608 | tf_op jit(solution)/shard_map/ppermute | solution.py:216
  262.8 22.8 %collective-permute-start.34 = (bf16[80,1920]{1,0:T(8,128)(2,1)S(1)}, bf16[80,1920]{1,0:T(8,128)(2,1)S(1)}, u32[]{:S(2)}, u32[]{:S(2)}) collective-permute-start(bf16[80,1920]{1,0:T(8,128)(2,1)S(1)} %bitcast.80), channel_id=1, source_target_pairs={{0,7},{1,6},{2,5},{3,4},{4,3},{5,2},{6,1},{7,0},{8,15},{9,14},{10,... | collective-permute-start | bytes 921608 | tf_op jit(solution)/shard_map/ppermute | solution.py:216
  271.0 32.4 %collective-permute-start.22 = (bf16[80,1920]{1,0:T(8,128)(2,1)S(1)}, bf16[80,1920]{1,0:T(8,128)(2,1)S(1)}, u32[]{:S(2)}, u32[]{:S(2)}) collective-permute-start(bf16[80,1920]{1,0:T(8,128)(2,1)S(1)} %bitcast.83), channel_id=1, source_target_pairs={{0,4},{1,5},{2,6},{3,7},{4,0},{5,1},{6,2},{7,3},{8,12},{9,13},{10,... | collective-permute-start | bytes 921608 | tf_op jit(solution)/shard_map/ppermute | solution.py:216
  271.1 32.3 %collective-permute-start.12 = (bf16[80,1920]{1,0:T(8,128)(2,1)S(1)}, bf16[80,1920]{1,0:T(8,128)(2,1)S(1)}, u32[]{:S(2)}, u32[]{:S(2)}) collective-permute-start(bf16[80,1920]{1,0:T(8,128)(2,1)S(1)} %bitcast.78), channel_id=1, source_target_pairs={{0,2},{1,3},{2,0},{3,1},{4,6},{5,7},{6,4},{7,5},{8,10},{9,11},{10,... | collective-permute-start | bytes 921608 | tf_op jit(solution)/shard_map/ppermute | solution.py:216
  282.3 21.1 %collective-permute-start.11 = (bf16[80,1920]{1,0:T(8,128)(2,1)}, bf16[80,1920]{1,0:T(8,128)(2,1)S(1)}, u32[]{:S(2)}, u32[]{:S(2)}) collective-permute-start(bf16[80,1920]{1,0:T(8,128)(2,1)} %bitcast.77), channel_id=1, source_target_pairs={{0,1},{1,0},{2,3},{3,2},{4,5},{5,4},{6,7},{7,6},{8,9},{9,8},{10,11... | collective-permute-start | bytes 921608 | tf_op jit(solution)/shard_map/ppermute | solution.py:216
  309.1 29.9 %all-to-all-start = ((f32[32,24,128]{2,1,0:T(8,128)}), f32[32,24,128]{2,1,0:T(8,128)S(1)}, u32[]{:S(2)}, u32[]{:S(2)}) async-start(f32[32,24,128]{2,1,0:T(8,128)} %get-tuple-element.109), calls=%async_computation | async-start | bytes 786432 | tf_op jit(solution)/shard_map/all_to_all | solution.py:310
  (27 other events, 303.6 us)

commit v2 on v1

--- a/solution.py
+++ b/solution.py
@@ -81,42 +81,51 @@
         out[:, width:] = (dot(pick, cot) * weight).astype(BF)
 
 
-def expert_kernel(width, near_ref, far_ref, gate_ref, up_ref, down_ref, *outs):
-    gate, up, down = gate_ref[0], up_ref[0], down_ref[0]
-    ff = gate.shape[1]
+def prepare_kernel(gate_ref, up_ref, down_ref, both_ref, turned_ref, down_out):
+    ff = gate_ref.shape[2]
+    both_ref[0, :, :ff] = gate_ref[0]
+    both_ref[0, :, ff:] = up_ref[0]
+    turned_ref[0, :ff, :] = gate_ref[0].T
+    turned_ref[0, ff:, :] = up_ref[0].T
+    down_out[0] = down_ref[0].T
+
+
+def expert_kernel(width, near_ref, far_ref, both_ref, turned_ref, down_ref, *outs):
+    both, turned, down = both_ref[0], turned_ref[0], down_ref[0]
+    ff = down.shape[1]
     for rows_ref, (back_ref, hidden_ref, pre_ref) in ((near_ref, outs[:3]), (far_ref, outs[3:])):
-        rows = rows_ref[0, :, :width]
-        gate_pre = dot(rows, gate)
-        up_one = dot(rows, up) + 1.0
-        grad = dot(rows_ref[0, :, width:], down, 1, 1)
+        pre = dot(rows_ref[0, :, :width], both)
+        gate_pre, up_one = pre[:, :ff], pre[:, ff:] + 1.0
+        grad = dot(rows_ref[0, :, width:], down)
         squash = jax.nn.sigmoid(SWISH_SCALE * gate_pre)
         swish = gate_pre * squash
         hidden = (swish * up_one).astype(BF)
         score = jnp.sum(grad * hidden.astype(F32), axis=1, keepdims=True)
         slope = squash + SWISH_SCALE * swish * (1.0 - squash)
-        pre_gate = (grad * up_one * slope).astype(BF)
-        pre_up = (grad * swish).astype(BF)
         hidden_ref[0] = hidden
-        pre_ref[0, :, :ff] = pre_gate
-        pre_ref[0, :, ff:] = pre_up
-        back = dot(pre_gate, gate, 1, 1) + dot(pre_up, up, 1, 1)
-        back_ref[0, :, :width] = back.astype(BF)
-        lane = lax.broadcasted_iota(jnp.int32, (rows.shape[0], LANES), 1)
+        pre_ref[0, :, :ff] = (grad * up_one * slope).astype(BF)
+        pre_ref[0, :, ff:] = (grad * swish).astype(BF)
+        back_ref[0, :, :width] = dot(pre_ref[0], turned).astype(BF)
+        lane = lax.broadcasted_iota(jnp.int32, (score.shape[0], LANES), 1)
         back_ref[0, :, width:] = jnp.where(lane == 0, score, 0.0).astype(BF)
 
 
 def weight_kernel(count, *refs):
-    rows, ups = refs[:count], refs[count : 2 * count]
-    hiddens, pres = refs[2 * count : 3 * count], refs[3 * count : 4 * count]
-    gate_out, up_out, down_out = refs[-3:]
+    gate_out, up_out, down_out, rows_ref, ups_ref, hid_ref, pre_ref = refs[-7:]
     ff = gate_out.shape[2]
-    both = sum(dot(r[0], p[0], 0, 0) for r, p in zip(rows, pres))
+    for n, joined in enumerate((rows_ref, ups_ref, hid_ref, pre_ref)):
+        at = 0
+        for piece in refs[n * count : (n + 1) * count]:
+            joined[at : at + piece.shape[1]] = piece[0]
+            at += piece.shape[1]
+    both = dot(rows_ref[...], pre_ref[...], 0, 0)
     gate_out[0] = both[:, :ff].astype(BF)
     up_out[0] = both[:, ff:].astype(BF)
-    down_out[0] = sum(dot(h[0], u[0], 0, 0) for h, u in zip(hiddens, ups)).astype(BF)
-
-
-def tail_kernel(local, cap, experts, shard, count, *refs):
+    down_out[0] = dot(hid_ref[...], ups_ref[...], 0, 0).astype(BF)
+
+
+def tail_kernel(local, cap, experts, shard, packed, sources, *refs):
+    count = len(sources)
     pieces = refs[:count]
     rank_ref, gates_ref, tokens_ref, cot_ref, labels_ref, gain_ref, router_ref = refs[count : count + 7]
     grad_ref, part_ref, score_ref = refs[count + 7 :]
@@ -127,7 +136,7 @@
     router = dot(permutation(labels_ref, experts), router_ref[...]).astype(BF)
     score_ref[...] = jnp.zeros(score_ref.shape, F32)
     back = None
-    for s, piece in enumerate(pieces):
+    for s, piece in zip(sources, pieces):
         pick = slot_mask(rank, s * local, local, cap, 1).astype(F32).astype(BF)
         part = dot(pick, piece[:, :width])
         back = part if back is None else back + part
@@ -136,7 +145,7 @@
         slot = lax.broadcasted_iota(jnp.int32, hit.shape, 0)
         for e in range(local):
             mine = hit & (slot >= e * cap) & (slot < (e + 1) * cap)
-            score_ref[s * local + e : s * local + e + 1, :] = jnp.sum(
+            score_ref[s * local + e : s * local + e + 1, :] += jnp.sum(
                 jnp.where(mine, column, 0.0), axis=0, keepdims=True
             )
     score = score_ref[...]
@@ -146,12 +155,20 @@
     natural = dot(permutation(labels_ref, LANES), grad_logits.astype(BF), 0, 0)
     part_t = dot(natural.astype(BF), normed)
     gain_part = jnp.sum(grad_normed * scaled, axis=0, keepdims=True)
-    wide = part_ref.shape[1]
-    line = lax.broadcasted_iota(jnp.int32, (wide, width), 0)
-    part = jnp.where(line == experts, gain_part, part_t[:wide])
-    part_ref[...] = jnp.zeros(part_ref.shape, F32)
-    for d in range(part_ref.shape[0]):
-        part_ref[d, :, :shard] = part[:, d * shard : (d + 1) * shard]
+    line = lax.broadcasted_iota(jnp.int32, (LANES, width), 0)
+    part = jnp.where(line == experts, gain_part, part_t)
+    if packed:
+        columns = part.T
+        for d in range(part_ref.shape[0]):
+            first = d * shard
+            total = columns[first : first + 8]
+            for g in range(1, shard // 8):
+                total = total + pltpu.roll(columns[first + 8 * g : first + 8 * g + 8], g * (experts + 1), 1)
+            part_ref[d] = total
+    else:
+        part_ref[...] = jnp.zeros(part_ref.shape, F32)
+        for d in range(part_ref.shape[0]):
+            part_ref[d, :, :shard] = part[: part_ref.shape[1], d * shard : (d + 1) * shard]
     grad_scaled = grad_normed * gain
     correction = jnp.mean(grad_scaled * scaled, axis=1, keepdims=True)
     grad_ref[...] = (
@@ -159,29 +176,43 @@
     ).astype(BF)
 
 
-def add_kernel(*refs):
-    total = refs[0][...].astype(F32)
-    for ref in refs[1:-1]:
-        total = total + ref[...].astype(F32)
-    refs[-1][...] = total.astype(BF)
-
-
-def add_pieces(*terms, count):
-    local, _, cap, wide = terms[0][0].shape
-    block = (local, 1, cap, wide)
-    return pl.pallas_call(
-        add_kernel,
-        grid=(count,),
-        in_specs=[pl.BlockSpec(block, lambda i, at=at: (0, at + i, 0, 0)) for _, at in terms],
-        out_specs=pl.BlockSpec(block, lambda i: (0, i, 0, 0)),
-        out_shape=jax.ShapeDtypeStruct((local, count, cap, wide), BF),
-        name="add",
-    )(*[value for value, _ in terms])
+def sum_kernel(sizes, near_ref, other_ref, *outs):
+    count = sum(sizes)
+    at = 0
+    for size, leave, own in zip(sizes, outs[: len(sizes)], outs[len(sizes) :]):
+        for out, first in ((leave, count + at), (own, at)):
+            cut = slice(first, first + size)
+            out[0] = (near_ref[0, cut].astype(F32) + other_ref[0, cut].astype(F32)).astype(BF)
+        at += size
+
+
+def sum_group(near, other, sizes):
+    local, count, cap, wide = near.shape
+    spec = lambda size: pl.BlockSpec((1, size, cap, wide), lambda e: (e, 0, 0, 0))
+    outs = pl.pallas_call(
+        functools.partial(sum_kernel, sizes),
+        grid=(local,),
+        in_specs=[spec(count)] * 2,
+        out_specs=[spec(size) for size in sizes] * 2,
+        out_shape=[jax.ShapeDtypeStruct((local, size, cap, wide), BF) for size in sizes] * 2,
+        name="sum",
+    )(near, other)
+    return outs[: len(sizes)], outs[len(sizes) :]
+
+
+def finish_kernel(experts, in_ref, router_ref, gain_ref):
+    total = jnp.sum(in_ref[...], axis=0)
+    turned = jnp.concatenate([total] * (LANES // 8), axis=0).T
+    for g in range(router_ref.shape[0] // 8):
+        block = pltpu.roll(total, -g * (experts + 1) % LANES, 1) if g else total
+        router_ref[8 * g : 8 * g + 8, :] = block[:, :experts]
+        line = g * (experts + 1) + experts
+        gain_ref[:, 8 * g : 8 * g + 8] = turned[line : line + 1, 8 * g : 8 * g + 8]
 
 
 def plan(n_ctx):
     if n_ctx == 8:
-        return ((0, 1, 2, 4), (3, 5), (6, 7)), (((4,), (0,), (1, 2)), ((5,), (3,)), ((6,), (7,)))
+        return ((0, 1, 2, 4), (3, 5), (6, 7)), (((0,), (1, 2), (4,)), ((3,), (5,)), ((6,), (7,)))
     half, quarter = n_ctx // 2, n_ctx // 4
     groups = (tuple(range(half)), tuple(range(half, half + quarter)), tuple(range(half + quarter, n_ctx)))
     return groups, tuple((g,) for g in groups)
@@ -225,6 +256,18 @@
     arrived = {s: across(messages[s], s) if s else messages[s] for s in range(n_ctx)}
     crossed = {s: chip(arrived[s]) for s in range(n_ctx)}
 
+    turn = lambda *shape: pl.BlockSpec((1, *shape), lambda e: (e, 0, 0))
+    turned_shapes = ((width, 2 * ff), (2 * ff, width), (width, ff))
+    prepared = pl.pallas_call(
+        prepare_kernel,
+        grid=(local,),
+        in_specs=[turn(width, ff)] * 2 + [turn(ff, width)],
+        out_specs=[turn(*t) for t in turned_shapes],
+        out_shape=[jax.ShapeDtypeStruct((local, *t), BF) for t in turned_shapes],
+        compiler_params=limit,
+        name="prepare",
+    )(gate_weight, up_weight, down_weight)
+
     def expert_pass(near, far):
         rows = near.shape[1]
         spec = lambda *shape: pl.BlockSpec((1, *shape), lambda e: (e, 0, 0))
@@ -233,13 +276,13 @@
         return pl.pallas_call(
             functools.partial(expert_kernel, width),
             grid=(local,),
-            in_specs=[spec(rows, 2 * width)] * 2 + [spec(width, ff)] * 2 + [spec(ff, width)],
+            in_specs=[spec(rows, 2 * width)] * 2 + [spec(width, 2 * ff), spec(2 * ff, width), spec(width, ff)],
             out_specs=[spec(*o) for o in outs],
             out_shape=[jax.ShapeDtypeStruct((local, *o), BF) for o in outs],
             compiler_params=limit,
             cost_estimate=pl.CostEstimate(flops=flops, bytes_accessed=16 * rows * width, transcendentals=0),
             name="expert",
-        )(near, far, gate_weight, up_weight, down_weight)
+        )(near, far, *prepared)
 
     done = []
     for group in groups:
@@ -248,18 +291,22 @@
         far = core(near)
         done.append((near, far, *expert_pass(near, far)))
 
-    returned = {}
+    sources, returned = [], []
     for g, group in enumerate(groups):
         split = lambda v: v.reshape(local, 2 * len(group), cap, wide)
         near, other = split(done[g][2]), split(core(done[g][5]))
-        for unit in units[g]:
-            first, size = group.index(unit[0]), len(unit)
-            leave = add_pieces((near, len(group) + first), (other, len(group) + first), count=size)
+        leaves, owns = sum_group(near, other, tuple(len(u) for u in units[g]))
+        for unit, leave, own in zip(units[g], leaves, owns):
             came = chip(leave)
+            if unit == (0,):
+                sources += [0, 0]
+                returned += [own.reshape(slots, wide), came.reshape(slots, wide)]
+                continue
             for i, s in enumerate(unit):
-                final = add_pieces((near, first + i), (other, first + i), (came, i), count=1)
+                final = (own[:, i].astype(F32) + came[:, i].astype(F32)).astype(BF)
                 final = final.reshape(slots, wide)
-                returned[s] = across(final, s) if s else final
+                sources.append(s)
+                returned.append(across(final, s) if s else final)
 
     near_rows = [d[0] for d in done] + [d[1] for d in done]
     hiddens = [d[3] for d in done] + [d[6] for d in done]
@@ -283,6 +330,7 @@
             + [pl.BlockSpec((1, ff, tile), lambda e: (e, 0, step))],
             out_shape=[jax.ShapeDtypeStruct((local, width, ff), BF)] * 2
             + [jax.ShapeDtypeStruct((local, ff, width), BF)],
+            scratch_shapes=[pltpu.VMEM((total, n), BF) for n in (tile, tile, ff, 2 * ff)],
             input_output_aliases={4 * count + i: i for i in range(len(carry))},
             compiler_params=limit,
             cost_estimate=pl.CostEstimate(
@@ -297,18 +345,34 @@
 
     devices = n_dp * n_ctx
     shard = width // devices
-    lines = -(-(experts + 1) // 8) * 8
+    packed = shard % 8 == 0 and shard // 8 * (experts + 1) <= LANES
+    lines = 8 if packed else -(-(experts + 1) // 8) * 8
     grad_input, part = pl.pallas_call(
-        functools.partial(tail_kernel, local, cap, experts, shard, n_ctx),
+        functools.partial(tail_kernel, local, cap, experts, shard, packed, tuple(sources)),
         out_shape=[jax.ShapeDtypeStruct((rows_here, width), BF), jax.ShapeDtypeStruct((devices, lines, LANES), F32)],
-        in_specs=vmem(n_ctx + 7),
+        in_specs=vmem(len(sources) + 7),
         out_specs=vmem(2),
         scratch_shapes=[pltpu.VMEM((LANES, rows_here), F32)],
         compiler_params=limit,
         name="tail",
-    )(*[returned[s] for s in range(n_ctx)], rank, gates, tokens, cotangent, labels, norm_gain, router)
-    part = jnp.sum(lax.all_to_all(part, ("dp", "ctx"), 0, 0, tiled=True), axis=0)
-    return (grad_input, gate_grad, up_grad, down_grad, part[:experts, :shard].T, part[experts, :shard])
+    )(*returned, rank, gates, tokens, cotangent, labels, norm_gain, router)
+    part = lax.all_to_all(part, ("dp", "ctx"), 0, 0, tiled=True)
+    if packed:
+        grad_router, grad_gain = pl.pallas_call(
+            functools.partial(finish_kernel, experts),
+            out_shape=[
+                jax.ShapeDtypeStruct((shard, experts), F32),
+                jax.ShapeDtypeStruct((1, shard), F32),
+            ],
+            in_specs=vmem(1),
+            out_specs=vmem(2),
+            name="finish",
+        )(part)
+        grad_gain = grad_gain.reshape(shard)
+    else:
+        part = jnp.sum(part, axis=0)
+        grad_router, grad_gain = part[:experts, :shard].T, part[experts, :shard]
+    return (grad_input, gate_grad, up_grad, down_grad, grad_router, grad_gain)
 
 
 def solution(mesh):

time: 341 us -> 292 us (0.86)
  waiting for transfers between devices: 164 us -> 117 us
  Pallas kernels: 109 us -> 86.6 us
  starting transfers between devices: 56.1 us -> 64.8 us
  local copies, waits for them, and re-layouts: 6.63 us -> 14.7 us
  other arithmetic: 3.06 us -> 6.85 us
    ppermute x14, waiting for transfers between devices: 85 us -> 50.8 us  [across(): return lax.ppermute(value, 'ctx', [(i, i ^ s) for i in range(n_ctx)])]
    ppermute x15, waiting for transfers between devices: 79.1 us -> 66.6 us  [chip(): return lax.ppermute(value, 'dp', [(i, i ^ 2) for i in range(n_dp)])]
    pallas_call x15 -> x5, Pallas kernels: 29.2 us -> 18.9 us  [the longest x1 8.7 us: body(): pl.pallas_call(prepare_kernel, grid=(local,), in_specs=[turn(width, ff)]...]
    unnamed x53 -> x32, local copies, waits for them, and re-layouts: 4.74 us -> 13.1 us
    ppermute x14, starting transfers between devices: 33.4 us -> 41.6 us  [across(): return lax.ppermute(value, 'ctx', [(i, i ^ s) for i in range(n_ctx)])]
    convert_element_type x0 -> x6, other arithmetic: none -> 6.54 us  [body(): final = (own[:, i].astype(F32) + came[:, i].astype(F32)).astype(BF)]
    pallas_call x2, Pallas kernels: 27.3 us -> 20.8 us  [weights(): pl.pallas_call(functools.partial(weight_kernel, count), grid=(local,), in...]
    pallas_call x3, Pallas kernels: 43.8 us -> 37.3 us  [expert_pass(): pl.pallas_call(functools.partial(expert_kernel, width), grid=(local,), in...]
  transfers between devices with their start and end apart: 36 -> 36, of which waited for: 15 -> 13; matrix products, arithmetic and copies ran while one was open for 1% -> 5% of each run, Pallas kernels for 29% -> 26%
where the time goes in v2:
time: 292 us; the launch traced here: 291 us
  waiting for transfers between devices  117 us (40%)
  Pallas kernels  86.6 us (30%)
  starting transfers between devices  64.8 us (22%)
  local copies, waits for them, and re-layouts  14.7 us (5%)
  other arithmetic  6.85 us (2%)
    ppermute x15, waiting for transfers between devices, chip(): return lax.ppermute(value, 'dp', [(i, i ^ 2) for i in range(n_dp)])  66.6 us
    ppermute x14, waiting for transfers between devices, across(): return lax.ppermute(value, 'ctx', [(i, i ^ s) for i in range(n_ctx)])  50.8 us
    ppermute x14, starting transfers between devices, across(): return lax.ppermute(value, 'ctx', [(i, i ^ s) for i in range(n_ctx)])  41.6 us
    pallas_call x3, Pallas kernels, expert_pass(): pl.pallas_call(functools.partial(expert_kernel, width), grid=(local,), in...  37.3 us
    pallas_call x2, Pallas kernels, weights(): pl.pallas_call(functools.partial(weight_kernel, count), grid=(local,), in...  20.8 us
    ppermute x15, starting transfers between devices, chip(): return lax.ppermute(value, 'dp', [(i, i ^ 2) for i in range(n_dp)])  18.9 us
    unnamed x32, local copies, waits for them, and re-layouts  13.1 us
    pallas_call x1, Pallas kernels, body(): pl.pallas_call(prepare_kernel, grid=(local,), in_specs=[turn(width, ff)]...  8.7 us
  transfers between devices with their start and end apart: 36, of which 13 were waited for; matrix products, arithmetic and copies ran while one was open for 5% of the time, Pallas kernels for 26%

profile of v2, /device:TPU:0, one launch (start us, length us, event | category | flops | bytes accessed | tf_op | source)
XLA Modules:
  0.0 291.2 jit_solution(1463078547568447472)
XLA Ops:
  1.4 4.3 %head.1 = (bf16[80,3584]{1,0:T(8,128)(2,1)}, bf16[80,3584]{1,0:T(8,128)(2,1)}, bf16[80,3584]{1,0:T(8,128)(2,1)}, bf16[80,3584]{1,0:T(8,128)(2,1)}, bf16[80,3584]...) custom-call(bf16[128,1792]{1,0:T(8,128)(2,1)} %refs_11_.1, ...), custom_call_target="tpu_custom_call" | custom-call | tf_op jit(solution)/shard_map/head/pallas_call | solution.py:236
  5.7 3.0 %collective-permute-start = (bf16[80,3584]{1,0:T(8,128)(2,1)}, bf16[80,3584]{1,0:T(8,128)(2,1)S(1)}, u32[]{:S(2)}, u32[]{:S(2)}) collective-permute-start(bf16[80,3584]{1,0:T(8,128)(2,1)} %get-tuple-element.78), channel_id=1, source_target_pairs={{0,1},{1,0},{2,3},{3,2},{4,5},{5,4},{6,7},{7,6},{8,9},{9,8},{10,11... | collective-permute-start | bytes 1720328 | tf_op jit(solution)/shard_map/ppermute | solution.py:247
  10.2 2.6 collective-permute-start.2
  14.3 7.5 %collective-permute-done = bf16[80,3584]{1,0:T(8,128)(2,1)S(1)} collective-permute-done((bf16[80,3584]{1,0:T(8,128)(2,1)}, bf16[80,3584]{1,0:T(8,128)(2,1)S(1)}, u32[]{:S(2)}, u32[]{:S(2)}) %collective-permute-start) | collective-permute-done | bytes 573472 | tf_op jit(solution)/shard_map/ppermute | solution.py:247
  23.5 11.9 %collective-permute-done.1 = bf16[80,3584]{1,0:T(8,128)(2,1)S(1)} collective-permute-done((bf16[80,3584]{1,0:T(8,128)(2,1)}, bf16[80,3584]{1,0:T(8,128)(2,1)S(1)}, u32[]{:S(2)}, u32[]{:S(2)}) %collective-permute-start.1) | collective-permute-done | bytes 573472 | tf_op jit(solution)/shard_map/ppermute | solution.py:247
  39.7 3.5 %collective-permute-start.16 = (bf16[80,3584]{1,0:T(8,128)(2,1)}, bf16[80,3584]{1,0:T(8,128)(2,1)S(1)}, u32[]{:S(2)}, u32[]{:S(2)}) collective-permute-start(bf16[80,3584]{1,0:T(8,128)(2,1)} %get-tuple-element.101), channel_id=1, source_target_pairs={{0,5},{1,4},{2,7},{3,6},{4,1},{5,0},{6,3},{7,2},{8,13},{9,12},{10,... | collective-permute-start | bytes 1720328 | tf_op jit(solution)/shard_map/ppermute | solution.py:247
  43.3 10.2 %collective-permute-done.5 = bf16[80,3584]{1,0:T(8,128)(2,1)S(1)} collective-permute-done((bf16[80,3584]{1,0:T(8,128)(2,1)S(1)}, bf16[80,3584]{1,0:T(8,128)(2,1)S(1)}, u32[]{:S(2)}, u32[]{:S(2)}) %collective-permute-start.5) | collective-permute-done | bytes 573472 | tf_op jit(solution)/shard_map/ppermute | solution.py:250
  53.4 10.3 %collective-permute-done.6 = bf16[80,3584]{1,0:T(8,128)(2,1)S(1)} collective-permute-done((bf16[80,3584]{1,0:T(8,128)(2,1)S(1)}, bf16[80,3584]{1,0:T(8,128)(2,1)S(1)}, u32[]{:S(2)}, u32[]{:S(2)}) %collective-permute-start.6) | collective-permute-done | bytes 573472 | tf_op jit(solution)/shard_map/ppermute | solution.py:250
  63.8 2.0 constant_dynamic-update-slice_fusion.7
  72.2 3.4 %collective-permute-start.26 = (bf16[80,3584]{1,0:T(8,128)(2,1)S(1)}, bf16[80,3584]{1,0:T(8,128)(2,1)S(1)}, u32[]{:S(2)}, u32[]{:S(2)}) collective-permute-start(bf16[80,3584]{1,0:T(8,128)(2,1)S(1)} %copy-done.10), channel_id=1, source_target_pairs={{0,7},{1,6},{2,5},{3,4},{4,3},{5,2},{6,1},{7,0},{8,15},{9,14},{10,... | collective-permute-start | bytes 1720328 | tf_op jit(solution)/shard_map/ppermute | solution.py:247
  77.6 11.9 %collective-permute-done.25 = bf16[80,3584]{1,0:T(8,128)(2,1)S(1)} collective-permute-done((bf16[80,3584]{1,0:T(8,128)(2,1)S(1)}, bf16[80,3584]{1,0:T(8,128)(2,1)S(1)}, u32[]{:S(2)}, u32[]{:S(2)}) %collective-permute-start.25) | collective-permute-done | bytes 573472 | tf_op jit(solution)/shard_map/ppermute | solution.py:247
  91.1 10.3 %collective-permute-done.26 = bf16[80,3584]{1,0:T(8,128)(2,1)S(1)} collective-permute-done((bf16[80,3584]{1,0:T(8,128)(2,1)S(1)}, bf16[80,3584]{1,0:T(8,128)(2,1)S(1)}, u32[]{:S(2)}, u32[]{:S(2)}) %collective-permute-start.26) | collective-permute-done | bytes 573472 | tf_op jit(solution)/shard_map/ppermute | solution.py:247
  104.0 12.0 %collective-permute-done.27 = bf16[80,3584]{1,0:T(8,128)(2,1)S(1)} collective-permute-done((bf16[80,3584]{1,0:T(8,128)(2,1)S(1)}, bf16[80,3584]{1,0:T(8,128)(2,1)S(1)}, u32[]{:S(2)}, u32[]{:S(2)}) %collective-permute-start.27) | collective-permute-done | bytes 573472 | tf_op jit(solution)/shard_map/ppermute | solution.py:250
  116.0 11.3 %collective-permute-done.28 = bf16[80,3584]{1,0:T(8,128)(2,1)S(1)} collective-permute-done((bf16[80,3584]{1,0:T(8,128)(2,1)S(1)}, bf16[80,3584]{1,0:T(8,128)(2,1)S(1)}, u32[]{:S(2)}, u32[]{:S(2)}) %collective-permute-start.28) | collective-permute-done | bytes 573472 | tf_op jit(solution)/shard_map/ppermute | solution.py:250
  127.6 8.7 %prepare.1 = (bf16[2,1792,768]{2,1,0:T(8,128)(2,1)}, bf16[2,768,1792]{2,1,0:T(8,128)(2,1)}, bf16[2,1792,384]{2,1,0:T(8,128)(2,1)}) custom-call(bf16[2,1792,384]{2,1,0:T(8,128)(2,1)} %gate_ref.1, bf16[2,1792,384]{2,1,0:T(8,128)(2,1)} %up_ref.1, bf16[2,384,1792]{2,1,0:T(8,128)(2,1)} %down_ref.1), custom_call_target="tpu_custom_call" | custom-call | tf_op jit(solution)/shard_map/prepare/pallas_call | solution.py:261
  137.8 10.4 %expert.4 = (bf16[2,160,1920]{2,1,0:T(8,128)(2,1)}, bf16[2,160,384]{2,1,0:T(8,128)(2,1)}, bf16[2,160,768]{2,1,0:T(8,128)(2,1)}, bf16[2,160,1920]{2,1,0:T(8,128)(...) custom-call(bf16[2,160,3584]{2,1,0:T(8,128)(2,1)} %copy-done, bf16[2,160,3584]{2,1,0:T(8,128)(2,1)} %copy-done.2, ...), custom_call_target="tpu_custom_call" | custom-call | flops 4404019200 | bytes 4587520 | tf_op jit(solution)/shard_map/expert/pallas_call | solution.py:276
  148.2 10.4 %expert.5 = (bf16[2,160,1920]{2,1,0:T(8,128)(2,1)}, bf16[2,160,384]{2,1,0:T(8,128)(2,1)}, bf16[2,160,768]{2,1,0:T(8,128)(2,1)}, bf16[2,160,1920]{2,1,0:T(8,128)(...) custom-call(bf16[2,160,3584]{2,1,0:T(8,128)(2,1)} %copy-done.1, ...), custom_call_target="tpu_custom_call" | custom-call | flops 4404019200 | bytes 4587520 | tf_op jit(solution)/shard_map/expert/pallas_call | solution.py:276
  159.2 16.5 %expert.3 = (bf16[2,320,1920]{2,1,0:T(8,128)(2,1)}, bf16[2,320,384]{2,1,0:T(8,128)(2,1)}, bf16[2,320,768]{2,1,0:T(8,128)(2,1)}, bf16[2,320,1920]{2,1,0:T(8,128)(...) custom-call(bf16[2,320,3584]{2,1,0:T(8,128)(2,1)} %constant_dynamic-update-slice_fusion.near_ref.refs_0_.refs_6_, ...), custom_call_target="tpu_custom_call" | custom-call | flops 8808038400 | bytes 9175040 | tf_op jit(solution)/shard_map/expert/pallas_call | solution.py:276
  175.8 2.5 sum.4
  180.3 2.5 sum.5
  184.9 3.8 %collective-permute-done.21 = bf16[2,1,40,1920]{3,2,1,0:T(8,128)(2,1)S(1)} collective-permute-done((bf16[2,1,40,1920]{3,2,1,0:T(8,128)(2,1)}, bf16[2,1,40,1920]{3,2,1,0:T(8,128)(2,1)S(1)}, u32[]{:S(2)}, u32[]{:S(2)}) %collective-permute-start.21) | collective-permute-done | bytes 307232 | tf_op jit(solution)/shard_map/ppermute | solution.py:250
  189.7 12.7 %collective-permute-start.22 = (bf16[80,1920]{1,0:T(8,128)(2,1)S(1)}, bf16[80,1920]{1,0:T(8,128)(2,1)}, u32[]{:S(2)}, u32[]{:S(2)}) collective-permute-start(bf16[80,1920]{1,0:T(8,128)(2,1)S(1)} %bitcast.58), channel_id=1, source_target_pairs={{0,3},{1,2},{2,1},{3,0},{4,7},{5,6},{6,5},{7,4},{8,11},{9,10},{10,... | collective-permute-start | bytes 921608 | tf_op jit(solution)/shard_map/ppermute | solution.py:247
  203.5 5.4 %collective-permute-start.24 = (bf16[80,1920]{1,0:T(8,128)(2,1)S(1)}, bf16[80,1920]{1,0:T(8,128)(2,1)}, u32[]{:S(2)}, u32[]{:S(2)}) collective-permute-start(bf16[80,1920]{1,0:T(8,128)(2,1)S(1)} %bitcast.59), channel_id=1, source_target_pairs={{0,5},{1,4},{2,7},{3,6},{4,1},{5,0},{6,3},{7,2},{8,13},{9,12},{10,... | collective-permute-start | bytes 921608 | tf_op jit(solution)/shard_map/ppermute | solution.py:247
  210.0 2.5 collective-permute-start.32
  213.9 3.5 %sum.3 = (bf16[2,1,40,1920]{3,2,1,0:T(8,128)(2,1)}, bf16[2,2,40,1920]{3,2,1,0:T(8,128)(2,1)}, bf16[2,1,40,1920]{3,2,1,0:T(8,128)(2,1)}, bf16[2,1,40,1920]{3,2,1,...) custom-call(bf16[2,8,40,1920]{3,2,1,0:T(8,128)(2,1)} %bitcast.36, ...), custom_call_target="tpu_custom_call" | custom-call | tf_op jit(solution)/shard_map/sum/pallas_call | solution.py:192
  220.7 18.1 %collective-permute-done.13 = bf16[2,1,40,1920]{3,2,1,0:T(8,128)(2,1)S(1)} collective-permute-done((bf16[2,1,40,1920]{3,2,1,0:T(8,128)(2,1)}, bf16[2,1,40,1920]{3,2,1,0:T(8,128)(2,1)S(1)}, u32[]{:S(2)}, u32[]{:S(2)}) %collective-permute-start.13) | collective-permute-done | bytes 307232 | tf_op jit(solution)/shard_map/ppermute | solution.py:250
  244.0 3.9 %collective-permute-start.14 = (bf16[80,1920]{1,0:T(8,128)(2,1)S(1)}, bf16[80,1920]{1,0:T(8,128)(2,1)S(1)}, u32[]{:S(2)}, u32[]{:S(2)}) collective-permute-start(bf16[80,1920]{1,0:T(8,128)(2,1)S(1)} %bitcast.62), channel_id=1, source_target_pairs={{0,4},{1,5},{2,6},{3,7},{4,0},{5,1},{6,2},{7,3},{8,12},{9,13},{10,... | collective-permute-start | bytes 921608 | tf_op jit(solution)/shard_map/ppermute | solution.py:247
  248.6 10.4 %shard_map.127 = (bf16[2,1792,384]{2,1,0:T(8,128)(2,1)}, bf16[2,1792,384]{2,1,0:T(8,128)(2,1)}, bf16[2,384,1792]{2,1,0:T(8,128)(2,1)}) custom-call(bf16[2,320,3584]{2,1,0:T(8,128)(2,1)} %constant_dynamic-update-slice_fusion.near_ref.refs_0_.refs_6_, bf16[2,160,3584]{2,1,0:T(8,128)(2,1)} %copy-done, bf16[2,160,3584]{2,1,0:T(8,128)(2,1)} %copy-done.1, ...), custom_call_target="tpu_custom_call" | custom-call | flops 5284823040 | bytes 9175040 | tf_op jit(solution)/shard_map/pallas_call | solution.py:325
  259.1 8.2 %collective-permute-done.14.refs_4_ = bf16[80,1920]{1,0:T(8,128)(2,1)S(1)} collective-permute-done((bf16[80,1920]{1,0:T(8,128)(2,1)S(1)}, bf16[80,1920]{1,0:T(8,128)(2,1)S(1)}, u32[]{:S(2)}, u32[]{:S(2)}) %collective-permute-start.14) | collective-permute-done | bytes 307232 | tf_op jit(solution)/shard_map/ppermute | solution.py:247
  268.2 5.3 %tail.1 = (bf16[128,1792]{1,0:T(8,128)(2,1)}, f32[32,8,128]{2,1,0:T(8,128)}) custom-call(bf16[80,1920]{1,0:T(8,128)(2,1)} %bitcast.63, bf16[80,1920]{1,0:T(8,128)(2,1)} %bitcast.64, bf16[80,1920]{1,0:T(8,128)(2,1)} %copy-done.8, bf16[80,1920]{1,0:T(8,128)(2,1)} %copy-done.9, bf16[80,1920]{1,0:T(8,128)(2,1)} %copy-done.7, ...), custom_call_target="tpu_custom_call" | custom-call | tf_op jit(solution)/shard_map/tail/pallas_call | solution.py:350
  273.6 3.5 %all-to-all-start = ((f32[32,8,128]{2,1,0:T(8,128)}), f32[32,8,128]{2,1,0:T(8,128)S(1)}, u32[]{:S(2)}, u32[]{:S(2)}) async-start(f32[32,8,128]{2,1,0:T(8,128)} %get-tuple-element.145), calls=%async_computation | async-start | bytes 262144 | tf_op jit(solution)/shard_map/all_to_all | solution.py:359
  277.1 10.4 %shard_map.128 = (bf16[2,1792,384]{2,1,0:T(8,128)(2,1)}, bf16[2,1792,384]{2,1,0:T(8,128)(2,1)}, bf16[2,384,1792]{2,1,0:T(8,128)(2,1)}) custom-call(bf16[2,320,3584]{2,1,0:T(8,128)(2,1)} %constant_dynamic-update-slice_fusion.near_ref.refs_0_.refs_6_, bf16[2,160,3584]{2,1,0:T(8,128)(2,1)} %copy-done, ...), custom_call_target="tpu_custom_call", output_to_operand_aliasing={{0}: (24, {}), {1}: (25, {}), {2}: (26, {})} | custom-call | flops 5284823040 | bytes 9175040 | tf_op jit(solution)/shard_map/pallas_call | solution.py:325
  (96 shorter events, 47.1 us)
Async XLA Ops:
  8.6 26.8 %collective-permute-start.1 = (bf16[80,3584]{1,0:T(8,128)(2,1)}, bf16[80,3584]{1,0:T(8,128)(2,1)S(1)}, u32[]{:S(2)}, u32[]{:S(2)}) collective-permute-start(bf16[80,3584]{1,0:T(8,128)(2,1)} %get-tuple-element.79), channel_id=1, source_target_pairs={{0,2},{1,3},{2,0},{3,1},{4,6},{5,7},{6,4},{7,5},{8,10},{9,11},{10,... | collective-permute-start | bytes 1720328 | tf_op jit(solution)/shard_map/ppermute | solution.py:247
  10.2 27.6 %collective-permute-start.2 = (bf16[80,3584]{1,0:T(8,128)(2,1)}, bf16[80,3584]{1,0:T(8,128)(2,1)S(1)}, u32[]{:S(2)}, u32[]{:S(2)}) collective-permute-start(bf16[80,3584]{1,0:T(8,128)(2,1)} %get-tuple-element.80), channel_id=1, source_target_pairs={{0,4},{1,5},{2,6},{3,7},{4,0},{5,1},{6,2},{7,3},{8,12},{9,13},{10,... | collective-permute-start | bytes 1720328 | tf_op jit(solution)/shard_map/ppermute | solution.py:247
  12.8 26.9 %collective-permute-start.3 = (bf16[80,3584]{1,0:T(8,128)(2,1)}, bf16[80,3584]{1,0:T(8,128)(2,1)S(1)}, u32[]{:S(2)}, u32[]{:S(2)}) collective-permute-start(bf16[80,3584]{1,0:T(8,128)(2,1)} %get-tuple-element.81), channel_id=1, source_target_pairs={{0,16},{8,24},{16,0},{24,8},{1,17},{9,25},{17,1},{25,9},{2,18},{10... | collective-permute-start | bytes 1720328 | tf_op jit(solution)/shard_map/ppermute | solution.py:250
  21.8 21.4 %collective-permute-start.4 = (bf16[80,3584]{1,0:T(8,128)(2,1)S(1)}, bf16[80,3584]{1,0:T(8,128)(2,1)S(1)}, u32[]{:S(2)}, u32[]{:S(2)}) collective-permute-start(bf16[80,3584]{1,0:T(8,128)(2,1)S(1)} %collective-permute-done), channel_id=1, source_target_pairs={{0,16},{8,24},{16,0},{24,8},{1,17},{9,25},{17,1},{25,9},{2,18},{10... | collective-permute-start | bytes 1720328 | tf_op jit(solution)/shard_map/ppermute | solution.py:250
  35.5 18.0 %collective-permute-start.5 = (bf16[80,3584]{1,0:T(8,128)(2,1)S(1)}, bf16[80,3584]{1,0:T(8,128)(2,1)S(1)}, u32[]{:S(2)}, u32[]{:S(2)}) collective-permute-start(bf16[80,3584]{1,0:T(8,128)(2,1)S(1)} %collective-permute-done.1), channel_id=1, source_target_pairs={{0,16},{8,24},{16,0},{24,8},{1,17},{9,25},{17,1},{25,9},{2,18},{10... | collective-permute-start | bytes 1720328 | tf_op jit(solution)/shard_map/ppermute | solution.py:250
  37.8 25.9 %collective-permute-start.6 = (bf16[80,3584]{1,0:T(8,128)(2,1)S(1)}, bf16[80,3584]{1,0:T(8,128)(2,1)S(1)}, u32[]{:S(2)}, u32[]{:S(2)}) collective-permute-start(bf16[80,3584]{1,0:T(8,128)(2,1)S(1)} %collective-permute-done.2), channel_id=1, source_target_pairs={{0,16},{8,24},{16,0},{24,8},{1,17},{9,25},{17,1},{25,9},{2,18},{10... | collective-permute-start | bytes 1720328 | tf_op jit(solution)/shard_map/ppermute | solution.py:250
  39.3 36.3 %collective-permute-start.15 = (bf16[80,3584]{1,0:T(8,128)(2,1)}, bf16[80,3584]{1,0:T(8,128)(2,1)S(1)}, u32[]{:S(2)}, u32[]{:S(2)}) collective-permute-start(bf16[80,3584]{1,0:T(8,128)(2,1)} %get-tuple-element.100), channel_id=1, source_target_pairs={{0,3},{1,2},{2,1},{3,0},{4,7},{5,6},{6,5},{7,4},{8,11},{9,10},{10,... | collective-permute-start | bytes 1720328 | tf_op jit(solution)/shard_map/ppermute | solution.py:247
  39.7 37.4 %collective-permute-start.16 = (bf16[80,3584]{1,0:T(8,128)(2,1)}, bf16[80,3584]{1,0:T(8,128)(2,1)S(1)}, u32[]{:S(2)}, u32[]{:S(2)}) collective-permute-start(bf16[80,3584]{1,0:T(8,128)(2,1)} %get-tuple-element.101), channel_id=1, source_target_pairs={{0,5},{1,4},{2,7},{3,6},{4,1},{5,0},{6,3},{7,2},{8,13},{9,12},{10,... | collective-permute-start | bytes 1720328 | tf_op jit(solution)/shard_map/ppermute | solution.py:247
  71.8 87.3 %collective-permute-start.7 = (bf16[2,320,3584]{2,1,0:T(8,128)(2,1)}, bf16[2,320,3584]{2,1,0:T(8,128)(2,1)}, u32[]{:S(2)}, u32[]{:S(2)}) collective-permute-start(bf16[2,320,3584]{2,1,0:T(8,128)(2,1)} %constant_dynamic-update-slice_fusion.near_ref.refs_0_.refs_6_), channel_id=1, source_target_pairs={{0,8},{8,0},{16,24},{24,16},{1,9},{9,1},{17,25},{25,17},{2,10},{10... | collective-permute-start | bytes 13762568 | tf_op jit(solution)/shard_map/ppermute | solution.py:253
  72.2 29.2 %collective-permute-start.26 = (bf16[80,3584]{1,0:T(8,128)(2,1)S(1)}, bf16[80,3584]{1,0:T(8,128)(2,1)S(1)}, u32[]{:S(2)}, u32[]{:S(2)}) collective-permute-start(bf16[80,3584]{1,0:T(8,128)(2,1)S(1)} %copy-done.10), channel_id=1, source_target_pairs={{0,7},{1,6},{2,5},{3,4},{4,3},{5,2},{6,1},{7,0},{8,15},{9,14},{10,... | collective-permute-start | bytes 1720328 | tf_op jit(solution)/shard_map/ppermute | solution.py:247
  75.6 27.2 %collective-permute-start.17 = (bf16[80,3584]{1,0:T(8,128)(2,1)S(1)}, bf16[80,3584]{1,0:T(8,128)(2,1)S(1)}, u32[]{:S(2)}, u32[]{:S(2)}) collective-permute-start(bf16[80,3584]{1,0:T(8,128)(2,1)S(1)} %collective-permute-done.15), channel_id=1, source_target_pairs={{0,16},{8,24},{16,0},{24,8},{1,17},{9,25},{17,1},{25,9},{2,18},{10... | collective-permute-start | bytes 1720328 | tf_op jit(solution)/shard_map/ppermute | solution.py:250
  77.1 26.6 %collective-permute-start.18 = (bf16[80,3584]{1,0:T(8,128)(2,1)S(1)}, bf16[80,3584]{1,0:T(8,128)(2,1)S(1)}, u32[]{:S(2)}, u32[]{:S(2)}) collective-permute-start(bf16[80,3584]{1,0:T(8,128)(2,1)S(1)} %collective-permute-done.16), channel_id=1, source_target_pairs={{0,16},{8,24},{16,0},{24,8},{1,17},{9,25},{17,1},{25,9},{2,18},{10... | collective-permute-start | bytes 1720328 | tf_op jit(solution)/shard_map/ppermute | solution.py:250
  89.6 26.5 %collective-permute-start.27 = (bf16[80,3584]{1,0:T(8,128)(2,1)S(1)}, bf16[80,3584]{1,0:T(8,128)(2,1)S(1)}, u32[]{:S(2)}, u32[]{:S(2)}) collective-permute-start(bf16[80,3584]{1,0:T(8,128)(2,1)S(1)} %collective-permute-done.25), channel_id=1, source_target_pairs={{0,16},{8,24},{16,0},{24,8},{1,17},{9,25},{17,1},{25,9},{2,18},{10... | collective-permute-start | bytes 1720328 | tf_op jit(solution)/shard_map/ppermute | solution.py:250
  101.4 25.9 %collective-permute-start.28 = (bf16[80,3584]{1,0:T(8,128)(2,1)S(1)}, bf16[80,3584]{1,0:T(8,128)(2,1)S(1)}, u32[]{:S(2)}, u32[]{:S(2)}) collective-permute-start(bf16[80,3584]{1,0:T(8,128)(2,1)S(1)} %collective-permute-done.26), channel_id=1, source_target_pairs={{0,16},{8,24},{16,0},{24,8},{1,17},{9,25},{17,1},{25,9},{2,18},{10... | collective-permute-start | bytes 1720328 | tf_op jit(solution)/shard_map/ppermute | solution.py:250
  103.9 32.3 %collective-permute-start.19 = (bf16[2,160,3584]{2,1,0:T(8,128)(2,1)S(1)}, bf16[2,160,3584]{2,1,0:T(8,128)(2,1)S(1)}, u32[]{:S(2)}, u32[]{:S(2)}) collective-permute-start(bf16[2,160,3584]{2,1,0:T(8,128)(2,1)S(1)} %pad_maximum_fusion.near_ref.refs_1_.refs_7_), channel_id=1, source_target_pairs={{0,8},{8,0},{16,24},{24,16},{1,9},{9,1},{17,25},{25,17},{2,10},{10... | collective-permute-start | bytes 6881288 | tf_op jit(solution)/shard_map/ppermute | solution.py:253
  127.5 20.8 %collective-permute-start.29 = (bf16[2,160,3584]{2,1,0:T(8,128)(2,1)S(1)}, bf16[2,160,3584]{2,1,0:T(8,128)(2,1)}, u32[]{:S(2)}, u32[]{:S(2)}) collective-permute-start(bf16[2,160,3584]{2,1,0:T(8,128)(2,1)S(1)} %pad_maximum_fusion.1.near_ref.refs_2_.refs_8_), channel_id=1, source_target_pairs={{0,8},{8,0},{16,24},{24,16},{1,9},{9,1},{17,25},{25,17},{2,10},{10... | collective-permute-start | bytes 6881288 | tf_op jit(solution)/shard_map/ppermute | solution.py:253
  148.1 27.7 %collective-permute-start.20 = (bf16[2,160,1920]{2,1,0:T(8,128)(2,1)}, bf16[2,160,1920]{2,1,0:T(8,128)(2,1)}, u32[]{:S(2)}, u32[]{:S(2)}) collective-permute-start(bf16[2,160,1920]{2,1,0:T(8,128)(2,1)} %get-tuple-element.107), channel_id=1, source_target_pairs={{0,8},{8,0},{16,24},{24,16},{1,9},{9,1},{17,25},{25,17},{2,10},{10... | collective-permute-start | bytes 3686408 | tf_op jit(solution)/shard_map/ppermute | solution.py:253
  158.6 21.7 %collective-permute-start.30 = (bf16[2,160,1920]{2,1,0:T(8,128)(2,1)}, bf16[2,160,1920]{2,1,0:T(8,128)(2,1)}, u32[]{:S(2)}, u32[]{:S(2)}) collective-permute-start(bf16[2,160,1920]{2,1,0:T(8,128)(2,1)} %get-tuple-element.119), channel_id=1, source_target_pairs={{0,8},{8,0},{16,24},{24,16},{1,9},{9,1},{17,25},{25,17},{2,10},{10... | collective-permute-start | bytes 3686408 | tf_op jit(solution)/shard_map/ppermute | solution.py:253
  175.7 36.8 %collective-permute-start.8 = (bf16[2,320,1920]{2,1,0:T(8,128)(2,1)}, bf16[2,320,1920]{2,1,0:T(8,128)(2,1)S(1)}, u32[]{:S(2)}, u32[]{:S(2)}) collective-permute-start(bf16[2,320,1920]{2,1,0:T(8,128)(2,1)} %get-tuple-element.93), channel_id=1, source_target_pairs={{0,8},{8,0},{16,24},{24,16},{1,9},{9,1},{17,25},{25,17},{2,10},{10... | collective-permute-start | bytes 7372808 | tf_op jit(solution)/shard_map/ppermute | solution.py:253
  179.8 22.7 %collective-permute-start.23 = (bf16[2,1,40,1920]{3,2,1,0:T(8,128)(2,1)}, bf16[2,1,40,1920]{3,2,1,0:T(8,128)(2,1)S(1)}, u32[]{:S(2)}, u32[]{:S(2)}) collective-permute-start(bf16[2,1,40,1920]{3,2,1,0:T(8,128)(2,1)} %get-tuple-element.111), channel_id=1, source_target_pairs={{0,16},{8,24},{16,0},{24,8},{1,17},{9,25},{17,1},{25,9},{2,18},{10... | collective-permute-start | bytes 921608 | tf_op jit(solution)/shard_map/ppermute | solution.py:250
  182.9 26.0 %collective-permute-start.31 = (bf16[2,1,40,1920]{3,2,1,0:T(8,128)(2,1)}, bf16[2,1,40,1920]{3,2,1,0:T(8,128)(2,1)S(1)}, u32[]{:S(2)}, u32[]{:S(2)}) collective-permute-start(bf16[2,1,40,1920]{3,2,1,0:T(8,128)(2,1)} %get-tuple-element.121), channel_id=1, source_target_pairs={{0,16},{8,24},{16,0},{24,8},{1,17},{9,25},{17,1},{25,9},{2,18},{10... | collective-permute-start | bytes 921608 | tf_op jit(solution)/shard_map/ppermute | solution.py:250
  184.4 34.6 %collective-permute-start.33 = (bf16[2,1,40,1920]{3,2,1,0:T(8,128)(2,1)}, bf16[2,1,40,1920]{3,2,1,0:T(8,128)(2,1)}, u32[]{:S(2)}, u32[]{:S(2)}) collective-permute-start(bf16[2,1,40,1920]{3,2,1,0:T(8,128)(2,1)} %get-tuple-element.123), channel_id=1, source_target_pairs={{0,16},{8,24},{16,0},{24,8},{1,17},{9,25},{17,1},{25,9},{2,18},{10... | collective-permute-start | bytes 921608 | tf_op jit(solution)/shard_map/ppermute | solution.py:250
  189.7 54.2 %collective-permute-start.22 = (bf16[80,1920]{1,0:T(8,128)(2,1)S(1)}, bf16[80,1920]{1,0:T(8,128)(2,1)}, u32[]{:S(2)}, u32[]{:S(2)}) collective-permute-start(bf16[80,1920]{1,0:T(8,128)(2,1)S(1)} %bitcast.58), channel_id=1, source_target_pairs={{0,3},{1,2},{2,1},{3,0},{4,7},{5,6},{6,5},{7,4},{8,11},{9,10},{10,... | collective-permute-start | bytes 921608 | tf_op jit(solution)/shard_map/ppermute | solution.py:247
  203.5 44.4 %collective-permute-start.24 = (bf16[80,1920]{1,0:T(8,128)(2,1)S(1)}, bf16[80,1920]{1,0:T(8,128)(2,1)}, u32[]{:S(2)}, u32[]{:S(2)}) collective-permute-start(bf16[80,1920]{1,0:T(8,128)(2,1)S(1)} %bitcast.59), channel_id=1, source_target_pairs={{0,5},{1,4},{2,7},{3,6},{4,1},{5,0},{6,3},{7,2},{8,13},{9,12},{10,... | collective-permute-start | bytes 921608 | tf_op jit(solution)/shard_map/ppermute | solution.py:247
  210.0 38.5 %collective-permute-start.32 = (bf16[80,1920]{1,0:T(8,128)(2,1)S(1)}, bf16[80,1920]{1,0:T(8,128)(2,1)}, u32[]{:S(2)}, u32[]{:S(2)}) collective-permute-start(bf16[80,1920]{1,0:T(8,128)(2,1)S(1)} %bitcast.60), channel_id=1, source_target_pairs={{0,6},{1,7},{2,4},{3,5},{4,2},{5,3},{6,0},{7,1},{8,14},{9,15},{10,... | collective-permute-start | bytes 921608 | tf_op jit(solution)/shard_map/ppermute | solution.py:247
  217.5 23.7 %collective-permute-start.10 = (bf16[2,2,40,1920]{3,2,1,0:T(8,128)(2,1)}, bf16[2,2,40,1920]{3,2,1,0:T(8,128)(2,1)S(1)}, u32[]{:S(2)}, u32[]{:S(2)}) collective-permute-start(bf16[2,2,40,1920]{3,2,1,0:T(8,128)(2,1)} %get-tuple-element.97), channel_id=1, source_target_pairs={{0,16},{8,24},{16,0},{24,8},{1,17},{9,25},{17,1},{25,9},{2,18},{10... | collective-permute-start | bytes 1843208 | tf_op jit(solution)/shard_map/ppermute | solution.py:250
  219.0 19.7 %collective-permute-start.13 = (bf16[2,1,40,1920]{3,2,1,0:T(8,128)(2,1)}, bf16[2,1,40,1920]{3,2,1,0:T(8,128)(2,1)S(1)}, u32[]{:S(2)}, u32[]{:S(2)}) collective-permute-start(bf16[2,1,40,1920]{3,2,1,0:T(8,128)(2,1)} %get-tuple-element.99), channel_id=1, source_target_pairs={{0,16},{8,24},{16,0},{24,8},{1,17},{9,25},{17,1},{25,9},{2,18},{10... | collective-permute-start | bytes 921608 | tf_op jit(solution)/shard_map/ppermute | solution.py:250
  238.8 20.3 %collective-permute-start.34 = (bf16[80,1920]{1,0:T(8,128)(2,1)S(1)}, bf16[80,1920]{1,0:T(8,128)(2,1)S(1)}, u32[]{:S(2)}, u32[]{:S(2)}) collective-permute-start(bf16[80,1920]{1,0:T(8,128)(2,1)S(1)} %bitcast.61), channel_id=1, source_target_pairs={{0,7},{1,6},{2,5},{3,4},{4,3},{5,2},{6,1},{7,0},{8,15},{9,14},{10,... | collective-permute-start | bytes 921608 | tf_op jit(solution)/shard_map/ppermute | solution.py:247
  241.2 17.9 %collective-permute-start.9 = (bf16[2,1,40,1920]{3,2,1,0:T(8,128)(2,1)}, bf16[2,1,40,1920]{3,2,1,0:T(8,128)(2,1)S(1)}, u32[]{:S(2)}, u32[]{:S(2)}) collective-permute-start(bf16[2,1,40,1920]{3,2,1,0:T(8,128)(2,1)} %get-tuple-element.95), channel_id=1, source_target_pairs={{0,16},{8,24},{16,0},{24,8},{1,17},{9,25},{17,1},{25,9},{2,18},{10... | collective-permute-start | bytes 921608 | tf_op jit(solution)/shard_map/ppermute | solution.py:250
  244.0 23.3 %collective-permute-start.14 = (bf16[80,1920]{1,0:T(8,128)(2,1)S(1)}, bf16[80,1920]{1,0:T(8,128)(2,1)S(1)}, u32[]{:S(2)}, u32[]{:S(2)}) collective-permute-start(bf16[80,1920]{1,0:T(8,128)(2,1)S(1)} %bitcast.62), channel_id=1, source_target_pairs={{0,4},{1,5},{2,6},{3,7},{4,0},{5,1},{6,2},{7,3},{8,12},{9,13},{10,... | collective-permute-start | bytes 921608 | tf_op jit(solution)/shard_map/ppermute | solution.py:247
  247.9 19.4 %collective-permute-start.11 = (bf16[80,1920]{1,0:T(8,128)(2,1)S(1)}, bf16[80,1920]{1,0:T(8,128)(2,1)S(1)}, u32[]{:S(2)}, u32[]{:S(2)}) collective-permute-start(bf16[80,1920]{1,0:T(8,128)(2,1)S(1)} %bitcast.57), channel_id=1, source_target_pairs={{0,1},{1,0},{2,3},{3,2},{4,5},{5,4},{6,7},{7,6},{8,9},{9,8},{10,11... | collective-permute-start | bytes 921608 | tf_op jit(solution)/shard_map/ppermute | solution.py:247
  248.4 18.9 %collective-permute-start.12 = (bf16[80,1920]{1,0:T(8,128)(2,1)S(1)}, bf16[80,1920]{1,0:T(8,128)(2,1)S(1)}, u32[]{:S(2)}, u32[]{:S(2)}) collective-permute-start(bf16[80,1920]{1,0:T(8,128)(2,1)S(1)} %bitcast.56), channel_id=1, source_target_pairs={{0,2},{1,3},{2,0},{3,1},{4,6},{5,7},{6,4},{7,5},{8,10},{9,11},{10,... | collective-permute-start | bytes 921608 | tf_op jit(solution)/shard_map/ppermute | solution.py:247
  (16 other events, 150.3 us)

commit v3 on v2

--- a/solution.py
+++ b/solution.py
@@ -176,38 +176,25 @@
     ).astype(BF)
 
 
-def sum_kernel(sizes, near_ref, other_ref, *outs):
-    count = sum(sizes)
-    at = 0
-    for size, leave, own in zip(sizes, outs[: len(sizes)], outs[len(sizes) :]):
-        for out, first in ((leave, count + at), (own, at)):
+def sum_group(near, other, sizes):
+    count = near.shape[1] // 2
+    leaves, owns, at = [], [], 0
+    for size in sizes:
+        for out, first in ((leaves, count + at), (owns, at)):
             cut = slice(first, first + size)
-            out[0] = (near_ref[0, cut].astype(F32) + other_ref[0, cut].astype(F32)).astype(BF)
+            out.append((near[:, cut].astype(F32) + other[:, cut].astype(F32)).astype(BF))
         at += size
-
-
-def sum_group(near, other, sizes):
-    local, count, cap, wide = near.shape
-    spec = lambda size: pl.BlockSpec((1, size, cap, wide), lambda e: (e, 0, 0, 0))
-    outs = pl.pallas_call(
-        functools.partial(sum_kernel, sizes),
-        grid=(local,),
-        in_specs=[spec(count)] * 2,
-        out_specs=[spec(size) for size in sizes] * 2,
-        out_shape=[jax.ShapeDtypeStruct((local, size, cap, wide), BF) for size in sizes] * 2,
-        name="sum",
-    )(near, other)
-    return outs[: len(sizes)], outs[len(sizes) :]
+    return lax.optimization_barrier((leaves, owns))
 
 
 def finish_kernel(experts, in_ref, router_ref, gain_ref):
     total = jnp.sum(in_ref[...], axis=0)
     turned = jnp.concatenate([total] * (LANES // 8), axis=0).T
-    for g in range(router_ref.shape[0] // 8):
-        block = pltpu.roll(total, -g * (experts + 1) % LANES, 1) if g else total
-        router_ref[8 * g : 8 * g + 8, :] = block[:, :experts]
-        line = g * (experts + 1) + experts
-        gain_ref[:, 8 * g : 8 * g + 8] = turned[line : line + 1, 8 * g : 8 * g + 8]
+    for g in range(gain_ref.shape[1] // 8):
+        first = g * (experts + 1)
+        lanes = slice(8 * g, 8 * g + 8)
+        router_ref[:, lanes] = turned[first : first + experts, lanes]
+        gain_ref[:, lanes] = turned[first + experts : first + experts + 1, lanes]
 
 
 def plan(n_ctx):
@@ -361,14 +348,14 @@
         grad_router, grad_gain = pl.pallas_call(
             functools.partial(finish_kernel, experts),
             out_shape=[
-                jax.ShapeDtypeStruct((shard, experts), F32),
+                jax.ShapeDtypeStruct((experts, shard), F32),
                 jax.ShapeDtypeStruct((1, shard), F32),
             ],
             in_specs=vmem(1),
             out_specs=vmem(2),
             name="finish",
         )(part)
-        grad_gain = grad_gain.reshape(shard)
+        grad_router, grad_gain = grad_router.T, grad_gain.reshape(shard)
     else:
         part = jnp.sum(part, axis=0)
         grad_router, grad_gain = part[:experts, :shard].T, part[experts, :shard]

time: 292 us -> 282 us (0.966)
  Pallas kernels: 86.6 us -> 78.1 us
  starting transfers between devices: 64.8 us -> 69.1 us
  other arithmetic: 6.85 us -> 2.81 us
    pallas_call x3 -> x0, Pallas kernels: 8.58 us -> none  [sum_group(): pl.pallas_call(functools.partial(sum_kernel, sizes), grid=(local,), in_sp...]
    convert_element_type x6, other arithmetic: 6.54 us -> 0.56 us  [body(): final = (own[:, i].astype(F32) + came[:, i].astype(F32)).astype(BF)]
    ppermute x14, starting transfers between devices: 41.6 us -> 45.9 us  [across(): return lax.ppermute(value, 'ctx', [(i, i ^ s) for i in range(n_ctx)])]
    unnamed x32 -> x41, local copies, waits for them, and re-layouts: 13.1 us -> 10.1 us
  transfers between devices with their start and end apart: 36 -> 36, of which waited for: 13 -> 13; matrix products, arithmetic and copies ran while one was open for 5% -> 4% of each run, Pallas kernels for 26% -> 24%
where the time goes in v3:
time: 282 us; the launch traced here: 281 us
  waiting for transfers between devices  119 us (42%)
  Pallas kernels  78.1 us (28%)
  starting transfers between devices  69.1 us (25%)
  local copies, waits for them, and re-layouts  11.8 us (4%)
    ppermute x15, waiting for transfers between devices, chip(): return lax.ppermute(value, 'dp', [(i, i ^ 2) for i in range(n_dp)])  69.1 us
    ppermute x14, waiting for transfers between devices, across(): return lax.ppermute(value, 'ctx', [(i, i ^ s) for i in range(n_ctx)])  49.4 us
    ppermute x14, starting transfers between devices, across(): return lax.ppermute(value, 'ctx', [(i, i ^ s) for i in range(n_ctx)])  45.9 us
    pallas_call x3, Pallas kernels, expert_pass(): pl.pallas_call(functools.partial(expert_kernel, width), grid=(local,), in...  37.3 us
    pallas_call x2, Pallas kernels, weights(): pl.pallas_call(functools.partial(weight_kernel, count), grid=(local,), in...  20.9 us
    ppermute x15, starting transfers between devices, chip(): return lax.ppermute(value, 'dp', [(i, i ^ 2) for i in range(n_dp)])  19 us
    unnamed x41, local copies, waits for them, and re-layouts  10.1 us
    pallas_call x1, Pallas kernels, body(): pl.pallas_call(prepare_kernel, grid=(local,), in_specs=[turn(width, ff)]...  8.71 us
  transfers between devices with their start and end apart: 36, of which 13 were waited for; matrix products, arithmetic and copies ran while one was open for 4% of the time, Pallas kernels for 24%

profile of v3, /device:TPU:0, one launch (start us, length us, event | category | flops | bytes accessed | tf_op | source)
XLA Modules:
  0.0 281.3 jit_solution(1816122631284479435)
XLA Ops:
  1.4 4.3 %head.1 = (bf16[80,3584]{1,0:T(8,128)(2,1)}, bf16[80,3584]{1,0:T(8,128)(2,1)}, bf16[80,3584]{1,0:T(8,128)(2,1)}, bf16[80,3584]{1,0:T(8,128)(2,1)}, bf16[80,3584]...) custom-call(bf16[128,1792]{1,0:T(8,128)(2,1)} %refs_11_.1, ...), custom_call_target="tpu_custom_call" | custom-call | tf_op jit(solution)/shard_map/head/pallas_call | solution.py:223
  5.7 3.0 %collective-permute-start = (bf16[80,3584]{1,0:T(8,128)(2,1)}, bf16[80,3584]{1,0:T(8,128)(2,1)S(1)}, u32[]{:S(2)}, u32[]{:S(2)}) collective-permute-start(bf16[80,3584]{1,0:T(8,128)(2,1)} %get-tuple-element.78), channel_id=1, source_target_pairs={{0,1},{1,0},{2,3},{3,2},{4,5},{5,4},{6,7},{7,6},{8,9},{9,8},{10,11... | collective-permute-start | bytes 1720328 | tf_op jit(solution)/shard_map/ppermute | solution.py:234
  8.7 1.6 collective-permute-start.1
  10.2 2.6 collective-permute-start.2
  14.3 7.5 %collective-permute-done = bf16[80,3584]{1,0:T(8,128)(2,1)S(1)} collective-permute-done((bf16[80,3584]{1,0:T(8,128)(2,1)}, bf16[80,3584]{1,0:T(8,128)(2,1)S(1)}, u32[]{:S(2)}, u32[]{:S(2)}) %collective-permute-start) | collective-permute-done | bytes 573472 | tf_op jit(solution)/shard_map/ppermute | solution.py:234
  21.8 1.7 collective-permute-start.4
  23.6 11.9 %collective-permute-done.1 = bf16[80,3584]{1,0:T(8,128)(2,1)S(1)} collective-permute-done((bf16[80,3584]{1,0:T(8,128)(2,1)}, bf16[80,3584]{1,0:T(8,128)(2,1)S(1)}, u32[]{:S(2)}, u32[]{:S(2)}) %collective-permute-start.1) | collective-permute-done | bytes 573472 | tf_op jit(solution)/shard_map/ppermute | solution.py:234
  39.7 3.5 %collective-permute-start.16 = (bf16[80,3584]{1,0:T(8,128)(2,1)}, bf16[80,3584]{1,0:T(8,128)(2,1)S(1)}, u32[]{:S(2)}, u32[]{:S(2)}) collective-permute-start(bf16[80,3584]{1,0:T(8,128)(2,1)} %get-tuple-element.101), channel_id=1, source_target_pairs={{0,5},{1,4},{2,7},{3,6},{4,1},{5,0},{6,3},{7,2},{8,13},{9,12},{10,... | collective-permute-start | bytes 1720328 | tf_op jit(solution)/shard_map/ppermute | solution.py:234
  43.3 10.2 %collective-permute-done.5 = bf16[80,3584]{1,0:T(8,128)(2,1)S(1)} collective-permute-done((bf16[80,3584]{1,0:T(8,128)(2,1)S(1)}, bf16[80,3584]{1,0:T(8,128)(2,1)S(1)}, u32[]{:S(2)}, u32[]{:S(2)}) %collective-permute-start.5) | collective-permute-done | bytes 573472 | tf_op jit(solution)/shard_map/ppermute | solution.py:237
  53.5 10.3 %collective-permute-done.6 = bf16[80,3584]{1,0:T(8,128)(2,1)S(1)} collective-permute-done((bf16[80,3584]{1,0:T(8,128)(2,1)S(1)}, bf16[80,3584]{1,0:T(8,128)(2,1)S(1)}, u32[]{:S(2)}, u32[]{:S(2)}) %collective-permute-start.6) | collective-permute-done | bytes 573472 | tf_op jit(solution)/shard_map/ppermute | solution.py:237
  63.8 1.9 constant_dynamic-update-slice_fusion.7
  72.0 3.4 %collective-permute-start.26 = (bf16[80,3584]{1,0:T(8,128)(2,1)S(1)}, bf16[80,3584]{1,0:T(8,128)(2,1)S(1)}, u32[]{:S(2)}, u32[]{:S(2)}) collective-permute-start(bf16[80,3584]{1,0:T(8,128)(2,1)S(1)} %copy-done.15), channel_id=1, source_target_pairs={{0,7},{1,6},{2,5},{3,4},{4,3},{5,2},{6,1},{7,0},{8,15},{9,14},{10,... | collective-permute-start | bytes 1720328 | tf_op jit(solution)/shard_map/ppermute | solution.py:234
  77.5 11.9 %collective-permute-done.25 = bf16[80,3584]{1,0:T(8,128)(2,1)S(1)} collective-permute-done((bf16[80,3584]{1,0:T(8,128)(2,1)S(1)}, bf16[80,3584]{1,0:T(8,128)(2,1)S(1)}, u32[]{:S(2)}, u32[]{:S(2)}) %collective-permute-start.25) | collective-permute-done | bytes 573472 | tf_op jit(solution)/shard_map/ppermute | solution.py:234
  90.9 10.3 %collective-permute-done.26 = bf16[80,3584]{1,0:T(8,128)(2,1)S(1)} collective-permute-done((bf16[80,3584]{1,0:T(8,128)(2,1)S(1)}, bf16[80,3584]{1,0:T(8,128)(2,1)S(1)}, u32[]{:S(2)}, u32[]{:S(2)}) %collective-permute-start.26) | collective-permute-done | bytes 573472 | tf_op jit(solution)/shard_map/ppermute | solution.py:234
  103.8 12.0 %collective-permute-done.27 = bf16[80,3584]{1,0:T(8,128)(2,1)S(1)} collective-permute-done((bf16[80,3584]{1,0:T(8,128)(2,1)S(1)}, bf16[80,3584]{1,0:T(8,128)(2,1)S(1)}, u32[]{:S(2)}, u32[]{:S(2)}) %collective-permute-start.27) | collective-permute-done | bytes 573472 | tf_op jit(solution)/shard_map/ppermute | solution.py:237
  115.9 11.3 %collective-permute-done.28 = bf16[80,3584]{1,0:T(8,128)(2,1)S(1)} collective-permute-done((bf16[80,3584]{1,0:T(8,128)(2,1)S(1)}, bf16[80,3584]{1,0:T(8,128)(2,1)S(1)}, u32[]{:S(2)}, u32[]{:S(2)}) %collective-permute-start.28) | collective-permute-done | bytes 573472 | tf_op jit(solution)/shard_map/ppermute | solution.py:237
  127.4 8.7 %prepare.1 = (bf16[2,1792,768]{2,1,0:T(8,128)(2,1)}, bf16[2,768,1792]{2,1,0:T(8,128)(2,1)}, bf16[2,1792,384]{2,1,0:T(8,128)(2,1)}) custom-call(bf16[2,1792,384]{2,1,0:T(8,128)(2,1)} %gate_ref.1, bf16[2,1792,384]{2,1,0:T(8,128)(2,1)} %up_ref.1, bf16[2,384,1792]{2,1,0:T(8,128)(2,1)} %down_ref.1), custom_call_target="tpu_custom_call" | custom-call | tf_op jit(solution)/shard_map/prepare/pallas_call | solution.py:248
  137.6 10.4 %expert.4 = (bf16[2,160,1920]{2,1,0:T(8,128)(2,1)}, bf16[2,160,384]{2,1,0:T(8,128)(2,1)}, bf16[2,160,768]{2,1,0:T(8,128)(2,1)}, bf16[2,160,1920]{2,1,0:T(8,128)(...) custom-call(bf16[2,160,3584]{2,1,0:T(8,128)(2,1)} %copy-done, bf16[2,160,3584]{2,1,0:T(8,128)(2,1)} %copy-done.2, ...), custom_call_target="tpu_custom_call" | custom-call | flops 4404019200 | bytes 4587520 | tf_op jit(solution)/shard_map/expert/pallas_call | solution.py:263
  148.0 10.4 %expert.5 = (bf16[2,160,1920]{2,1,0:T(8,128)(2,1)}, bf16[2,160,384]{2,1,0:T(8,128)(2,1)}, bf16[2,160,768]{2,1,0:T(8,128)(2,1)}, bf16[2,160,1920]{2,1,0:T(8,128)(...) custom-call(bf16[2,160,3584]{2,1,0:T(8,128)(2,1)} %copy-done.1, ...), custom_call_target="tpu_custom_call" | custom-call | flops 4404019200 | bytes 4587520 | tf_op jit(solution)/shard_map/expert/pallas_call | solution.py:263
  159.0 16.5 %expert.3 = (bf16[2,320,1920]{2,1,0:T(8,128)(2,1)}, bf16[2,320,384]{2,1,0:T(8,128)(2,1)}, bf16[2,320,768]{2,1,0:T(8,128)(2,1)}, bf16[2,320,1920]{2,1,0:T(8,128)(...) custom-call(bf16[2,320,3584]{2,1,0:T(8,128)(2,1)} %constant_dynamic-update-slice_fusion.near_ref.refs_0_.refs_6_, ...), custom_call_target="tpu_custom_call" | custom-call | flops 8808038400 | bytes 9175040 | tf_op jit(solution)/shard_map/expert/pallas_call | solution.py:263
  180.5 5.7 %collective-permute-done.21 = bf16[2,1,40,1920]{3,2,0,1:T(8,128)(2,1)S(1)} collective-permute-done((bf16[2,1,40,1920]{3,2,0,1:T(8,128)(2,1)S(1)}, bf16[2,1,40,1920]{3,2,0,1:T(8,128)(2,1)S(1)}, u32[]{:S(2)}, u32[]{:S(2)}) %collective-permute-start.21) | collective-permute-done | bytes 307232 | tf_op jit(solution)/shard_map/ppermute | solution.py:237
  186.3 12.7 %collective-permute-start.22 = (bf16[80,1920]{1,0:T(8,128)(2,1)S(1)}, bf16[80,1920]{1,0:T(8,128)(2,1)S(1)}, u32[]{:S(2)}, u32[]{:S(2)}) collective-permute-start(bf16[80,1920]{1,0:T(8,128)(2,1)S(1)} %bitcast.160), channel_id=1, source_target_pairs={{0,3},{1,2},{2,1},{3,0},{4,7},{5,6},{6,5},{7,4},{8,11},{9,10},{10,... | collective-permute-start | bytes 921608 | tf_op jit(solution)/shard_map/ppermute | solution.py:234
  199.1 6.4 %collective-permute-start.24 = (bf16[80,1920]{1,0:T(8,128)(2,1)S(1)}, bf16[80,1920]{1,0:T(8,128)(2,1)S(1)}, u32[]{:S(2)}, u32[]{:S(2)}) collective-permute-start(bf16[80,1920]{1,0:T(8,128)(2,1)S(1)} %bitcast.161), channel_id=1, source_target_pairs={{0,5},{1,4},{2,7},{3,6},{4,1},{5,0},{6,3},{7,2},{8,13},{9,12},{10,... | collective-permute-start | bytes 921608 | tf_op jit(solution)/shard_map/ppermute | solution.py:234
  205.6 2.5 collective-permute-start.32
  211.8 18.7 %collective-permute-done.13 = bf16[2,1,40,1920]{3,2,0,1:T(8,128)(2,1)S(1)} collective-permute-done((bf16[2,1,40,1920]{3,2,0,1:T(8,128)(2,1)S(1)}, bf16[2,1,40,1920]{3,2,0,1:T(8,128)(2,1)S(1)}, u32[]{:S(2)}, u32[]{:S(2)}) %collective-permute-start.13) | collective-permute-done | bytes 307232 | tf_op jit(solution)/shard_map/ppermute | solution.py:237
  233.6 7.6 %collective-permute-start.14 = (bf16[80,1920]{1,0:T(8,128)(2,1)S(1)}, bf16[80,1920]{1,0:T(8,128)(2,1)S(1)}, u32[]{:S(2)}, u32[]{:S(2)}) collective-permute-start(bf16[80,1920]{1,0:T(8,128)(2,1)S(1)} %bitcast.164), channel_id=1, source_target_pairs={{0,4},{1,5},{2,6},{3,7},{4,0},{5,1},{6,2},{7,3},{8,12},{9,13},{10,... | collective-permute-start | bytes 921608 | tf_op jit(solution)/shard_map/ppermute | solution.py:234
  241.7 10.5 %shard_map.127 = (bf16[2,1792,384]{2,1,0:T(8,128)(2,1)}, bf16[2,1792,384]{2,1,0:T(8,128)(2,1)}, bf16[2,384,1792]{2,1,0:T(8,128)(2,1)}) custom-call(bf16[2,320,3584]{2,1,0:T(8,128)(2,1)} %constant_dynamic-update-slice_fusion.near_ref.refs_0_.refs_6_, bf16[2,160,3584]{2,1,0:T(8,128)(2,1)} %copy-done, bf16[2,160,3584]{2,1,0:T(8,128)(2,1)} %copy-done.1, ...), custom_call_target="tpu_custom_call" | custom-call | flops 5284823040 | bytes 9175040 | tf_op jit(solution)/shard_map/pallas_call | solution.py:312
  252.3 6.9 %collective-permute-done.14.refs_4_ = bf16[80,1920]{1,0:T(8,128)(2,1)S(1)} collective-permute-done((bf16[80,1920]{1,0:T(8,128)(2,1)S(1)}, bf16[80,1920]{1,0:T(8,128)(2,1)S(1)}, u32[]{:S(2)}, u32[]{:S(2)}) %collective-permute-start.14) | collective-permute-done | bytes 307232 | tf_op jit(solution)/shard_map/ppermute | solution.py:234
  260.1 5.3 %tail.1 = (bf16[128,1792]{1,0:T(8,128)(2,1)}, f32[32,8,128]{2,1,0:T(8,128)}) custom-call(bf16[80,1920]{1,0:T(8,128)(2,1)} %bitcast.141, bf16[80,1920]{1,0:T(8,128)(2,1)} %bitcast.165, bf16[80,1920]{1,0:T(8,128)(2,1)} %copy-done.13, bf16[80,1920]{1,0:T(8,128)(2,1)} %copy-done.14, bf16[80,1920]{1,0:T(8,128)(2,1)} %copy-done.12, bf16[80,1920]{1,0:T(8,128)(2,1)} %copy-done.7, ...), custom_call_target="tpu_custom_call" | custom-call | tf_op jit(solution)/shard_map/tail/pallas_call | solution.py:337
  265.4 3.3 %all-to-all-start = ((f32[32,8,128]{2,1,0:T(8,128)}), f32[32,8,128]{2,1,0:T(8,128)S(1)}, u32[]{:S(2)}, u32[]{:S(2)}) async-start(f32[32,8,128]{2,1,0:T(8,128)} %get-tuple-element.145), calls=%async_computation | async-start | bytes 262144 | tf_op jit(solution)/shard_map/all_to_all | solution.py:346
  268.6 10.4 %shard_map.128 = (bf16[2,1792,384]{2,1,0:T(8,128)(2,1)}, bf16[2,1792,384]{2,1,0:T(8,128)(2,1)}, bf16[2,384,1792]{2,1,0:T(8,128)(2,1)}) custom-call(bf16[2,320,3584]{2,1,0:T(8,128)(2,1)} %constant_dynamic-update-slice_fusion.near_ref.refs_0_.refs_6_, bf16[2,160,3584]{2,1,0:T(8,128)(2,1)} %copy-done, ...), custom_call_target="tpu_custom_call", output_to_operand_aliasing={{0}: (24, {}), {1}: (25, {}), {2}: (26, {})} | custom-call | flops 5284823040 | bytes 9175040 | tf_op jit(solution)/shard_map/pallas_call | solution.py:312
  279.7 1.6 finish.1
  (108 shorter events, 35.3 us)
Async XLA Ops:
  8.7 26.8 %collective-permute-start.1 = (bf16[80,3584]{1,0:T(8,128)(2,1)}, bf16[80,3584]{1,0:T(8,128)(2,1)S(1)}, u32[]{:S(2)}, u32[]{:S(2)}) collective-permute-start(bf16[80,3584]{1,0:T(8,128)(2,1)} %get-tuple-element.79), channel_id=1, source_target_pairs={{0,2},{1,3},{2,0},{3,1},{4,6},{5,7},{6,4},{7,5},{8,10},{9,11},{10,... | collective-permute-start | bytes 1720328 | tf_op jit(solution)/shard_map/ppermute | solution.py:234
  10.2 27.6 %collective-permute-start.2 = (bf16[80,3584]{1,0:T(8,128)(2,1)}, bf16[80,3584]{1,0:T(8,128)(2,1)S(1)}, u32[]{:S(2)}, u32[]{:S(2)}) collective-permute-start(bf16[80,3584]{1,0:T(8,128)(2,1)} %get-tuple-element.80), channel_id=1, source_target_pairs={{0,4},{1,5},{2,6},{3,7},{4,0},{5,1},{6,2},{7,3},{8,12},{9,13},{10,... | collective-permute-start | bytes 1720328 | tf_op jit(solution)/shard_map/ppermute | solution.py:234
  12.8 26.9 %collective-permute-start.3 = (bf16[80,3584]{1,0:T(8,128)(2,1)}, bf16[80,3584]{1,0:T(8,128)(2,1)S(1)}, u32[]{:S(2)}, u32[]{:S(2)}) collective-permute-start(bf16[80,3584]{1,0:T(8,128)(2,1)} %get-tuple-element.81), channel_id=1, source_target_pairs={{0,16},{8,24},{16,0},{24,8},{1,17},{9,25},{17,1},{25,9},{2,18},{10... | collective-permute-start | bytes 1720328 | tf_op jit(solution)/shard_map/ppermute | solution.py:237
  21.8 21.4 %collective-permute-start.4 = (bf16[80,3584]{1,0:T(8,128)(2,1)S(1)}, bf16[80,3584]{1,0:T(8,128)(2,1)S(1)}, u32[]{:S(2)}, u32[]{:S(2)}) collective-permute-start(bf16[80,3584]{1,0:T(8,128)(2,1)S(1)} %collective-permute-done), channel_id=1, source_target_pairs={{0,16},{8,24},{16,0},{24,8},{1,17},{9,25},{17,1},{25,9},{2,18},{10... | collective-permute-start | bytes 1720328 | tf_op jit(solution)/shard_map/ppermute | solution.py:237
  35.5 18.0 %collective-permute-start.5 = (bf16[80,3584]{1,0:T(8,128)(2,1)S(1)}, bf16[80,3584]{1,0:T(8,128)(2,1)S(1)}, u32[]{:S(2)}, u32[]{:S(2)}) collective-permute-start(bf16[80,3584]{1,0:T(8,128)(2,1)S(1)} %collective-permute-done.1), channel_id=1, source_target_pairs={{0,16},{8,24},{16,0},{24,8},{1,17},{9,25},{17,1},{25,9},{2,18},{10... | collective-permute-start | bytes 1720328 | tf_op jit(solution)/shard_map/ppermute | solution.py:237
  37.8 25.9 %collective-permute-start.6 = (bf16[80,3584]{1,0:T(8,128)(2,1)S(1)}, bf16[80,3584]{1,0:T(8,128)(2,1)S(1)}, u32[]{:S(2)}, u32[]{:S(2)}) collective-permute-start(bf16[80,3584]{1,0:T(8,128)(2,1)S(1)} %collective-permute-done.2), channel_id=1, source_target_pairs={{0,16},{8,24},{16,0},{24,8},{1,17},{9,25},{17,1},{25,9},{2,18},{10... | collective-permute-start | bytes 1720328 | tf_op jit(solution)/shard_map/ppermute | solution.py:237
  39.3 36.1 %collective-permute-start.15 = (bf16[80,3584]{1,0:T(8,128)(2,1)}, bf16[80,3584]{1,0:T(8,128)(2,1)S(1)}, u32[]{:S(2)}, u32[]{:S(2)}) collective-permute-start(bf16[80,3584]{1,0:T(8,128)(2,1)} %get-tuple-element.100), channel_id=1, source_target_pairs={{0,3},{1,2},{2,1},{3,0},{4,7},{5,6},{6,5},{7,4},{8,11},{9,10},{10,... | collective-permute-start | bytes 1720328 | tf_op jit(solution)/shard_map/ppermute | solution.py:234
  39.7 37.2 %collective-permute-start.16 = (bf16[80,3584]{1,0:T(8,128)(2,1)}, bf16[80,3584]{1,0:T(8,128)(2,1)S(1)}, u32[]{:S(2)}, u32[]{:S(2)}) collective-permute-start(bf16[80,3584]{1,0:T(8,128)(2,1)} %get-tuple-element.101), channel_id=1, source_target_pairs={{0,5},{1,4},{2,7},{3,6},{4,1},{5,0},{6,3},{7,2},{8,13},{9,12},{10,... | collective-permute-start | bytes 1720328 | tf_op jit(solution)/shard_map/ppermute | solution.py:234
  71.7 87.3 %collective-permute-start.7 = (bf16[2,320,3584]{2,1,0:T(8,128)(2,1)}, bf16[2,320,3584]{2,1,0:T(8,128)(2,1)}, u32[]{:S(2)}, u32[]{:S(2)}) collective-permute-start(bf16[2,320,3584]{2,1,0:T(8,128)(2,1)} %constant_dynamic-update-slice_fusion.near_ref.refs_0_.refs_6_), channel_id=1, source_target_pairs={{0,8},{8,0},{16,24},{24,16},{1,9},{9,1},{17,25},{25,17},{2,10},{10... | collective-permute-start | bytes 13762568 | tf_op jit(solution)/shard_map/ppermute | solution.py:240
  71.7 17.7 %collective-permute-start.25 = (bf16[80,3584]{1,0:T(8,128)(2,1)S(1)}, bf16[80,3584]{1,0:T(8,128)(2,1)S(1)}, u32[]{:S(2)}, u32[]{:S(2)}) collective-permute-start(bf16[80,3584]{1,0:T(8,128)(2,1)S(1)} %copy-done.16), channel_id=1, source_target_pairs={{0,6},{1,7},{2,4},{3,5},{4,2},{5,3},{6,0},{7,1},{8,14},{9,15},{10,... | collective-permute-start | bytes 1720328 | tf_op jit(solution)/shard_map/ppermute | solution.py:234
  72.0 29.2 %collective-permute-start.26 = (bf16[80,3584]{1,0:T(8,128)(2,1)S(1)}, bf16[80,3584]{1,0:T(8,128)(2,1)S(1)}, u32[]{:S(2)}, u32[]{:S(2)}) collective-permute-start(bf16[80,3584]{1,0:T(8,128)(2,1)S(1)} %copy-done.15), channel_id=1, source_target_pairs={{0,7},{1,6},{2,5},{3,4},{4,3},{5,2},{6,1},{7,0},{8,15},{9,14},{10,... | collective-permute-start | bytes 1720328 | tf_op jit(solution)/shard_map/ppermute | solution.py:234
  75.4 27.2 %collective-permute-start.17 = (bf16[80,3584]{1,0:T(8,128)(2,1)S(1)}, bf16[80,3584]{1,0:T(8,128)(2,1)S(1)}, u32[]{:S(2)}, u32[]{:S(2)}) collective-permute-start(bf16[80,3584]{1,0:T(8,128)(2,1)S(1)} %collective-permute-done.15), channel_id=1, source_target_pairs={{0,16},{8,24},{16,0},{24,8},{1,17},{9,25},{17,1},{25,9},{2,18},{10... | collective-permute-start | bytes 1720328 | tf_op jit(solution)/shard_map/ppermute | solution.py:237
  76.9 26.7 %collective-permute-start.18 = (bf16[80,3584]{1,0:T(8,128)(2,1)S(1)}, bf16[80,3584]{1,0:T(8,128)(2,1)S(1)}, u32[]{:S(2)}, u32[]{:S(2)}) collective-permute-start(bf16[80,3584]{1,0:T(8,128)(2,1)S(1)} %collective-permute-done.16), channel_id=1, source_target_pairs={{0,16},{8,24},{16,0},{24,8},{1,17},{9,25},{17,1},{25,9},{2,18},{10... | collective-permute-start | bytes 1720328 | tf_op jit(solution)/shard_map/ppermute | solution.py:237
  89.4 26.5 %collective-permute-start.27 = (bf16[80,3584]{1,0:T(8,128)(2,1)S(1)}, bf16[80,3584]{1,0:T(8,128)(2,1)S(1)}, u32[]{:S(2)}, u32[]{:S(2)}) collective-permute-start(bf16[80,3584]{1,0:T(8,128)(2,1)S(1)} %collective-permute-done.25), channel_id=1, source_target_pairs={{0,16},{8,24},{16,0},{24,8},{1,17},{9,25},{17,1},{25,9},{2,18},{10... | collective-permute-start | bytes 1720328 | tf_op jit(solution)/shard_map/ppermute | solution.py:237
  101.2 25.9 %collective-permute-start.28 = (bf16[80,3584]{1,0:T(8,128)(2,1)S(1)}, bf16[80,3584]{1,0:T(8,128)(2,1)S(1)}, u32[]{:S(2)}, u32[]{:S(2)}) collective-permute-start(bf16[80,3584]{1,0:T(8,128)(2,1)S(1)} %collective-permute-done.26), channel_id=1, source_target_pairs={{0,16},{8,24},{16,0},{24,8},{1,17},{9,25},{17,1},{25,9},{2,18},{10... | collective-permute-start | bytes 1720328 | tf_op jit(solution)/shard_map/ppermute | solution.py:237
  103.7 32.4 %collective-permute-start.19 = (bf16[2,160,3584]{2,1,0:T(8,128)(2,1)S(1)}, bf16[2,160,3584]{2,1,0:T(8,128)(2,1)S(1)}, u32[]{:S(2)}, u32[]{:S(2)}) collective-permute-start(bf16[2,160,3584]{2,1,0:T(8,128)(2,1)S(1)} %pad_maximum_fusion.near_ref.refs_1_.refs_7_), channel_id=1, source_target_pairs={{0,8},{8,0},{16,24},{24,16},{1,9},{9,1},{17,25},{25,17},{2,10},{10... | collective-permute-start | bytes 6881288 | tf_op jit(solution)/shard_map/ppermute | solution.py:240
  127.3 20.7 %collective-permute-start.29 = (bf16[2,160,3584]{2,1,0:T(8,128)(2,1)S(1)}, bf16[2,160,3584]{2,1,0:T(8,128)(2,1)}, u32[]{:S(2)}, u32[]{:S(2)}) collective-permute-start(bf16[2,160,3584]{2,1,0:T(8,128)(2,1)S(1)} %pad_maximum_fusion.1.near_ref.refs_2_.refs_8_), channel_id=1, source_target_pairs={{0,8},{8,0},{16,24},{24,16},{1,9},{9,1},{17,25},{25,17},{2,10},{10... | collective-permute-start | bytes 6881288 | tf_op jit(solution)/shard_map/ppermute | solution.py:240
  148.0 27.7 %collective-permute-start.20 = (bf16[2,160,1920]{2,1,0:T(8,128)(2,1)}, bf16[2,160,1920]{2,1,0:T(8,128)(2,1)S(1)}, u32[]{:S(2)}, u32[]{:S(2)}) collective-permute-start(bf16[2,160,1920]{2,1,0:T(8,128)(2,1)} %get-tuple-element.107), channel_id=1, source_target_pairs={{0,8},{8,0},{16,24},{24,16},{1,9},{9,1},{17,25},{25,17},{2,10},{10... | collective-permute-start | bytes 3686408 | tf_op jit(solution)/shard_map/ppermute | solution.py:240
  158.4 19.7 %collective-permute-start.30 = (bf16[2,160,1920]{2,1,0:T(8,128)(2,1)}, bf16[2,160,1920]{2,1,0:T(8,128)(2,1)S(1)}, u32[]{:S(2)}, u32[]{:S(2)}) collective-permute-start(bf16[2,160,1920]{2,1,0:T(8,128)(2,1)} %get-tuple-element.119), channel_id=1, source_target_pairs={{0,8},{8,0},{16,24},{24,16},{1,9},{9,1},{17,25},{25,17},{2,10},{10... | collective-permute-start | bytes 3686408 | tf_op jit(solution)/shard_map/ppermute | solution.py:240
  175.5 32.7 %collective-permute-start.8 = (bf16[2,320,1920]{2,1,0:T(8,128)(2,1)}, bf16[2,320,1920]{2,1,0:T(8,128)(2,1)S(1)}, u32[]{:S(2)}, u32[]{:S(2)}) collective-permute-start(bf16[2,320,1920]{2,1,0:T(8,128)(2,1)} %get-tuple-element.93), channel_id=1, source_target_pairs={{0,8},{8,0},{16,24},{24,16},{1,9},{9,1},{17,25},{25,17},{2,10},{10... | collective-permute-start | bytes 7372808 | tf_op jit(solution)/shard_map/ppermute | solution.py:240
  177.5 21.5 %collective-permute-start.23 = (bf16[2,1,40,1920]{3,2,0,1:T(8,128)(2,1)S(1)}, bf16[2,1,40,1920]{3,2,0,1:T(8,128)(2,1)S(1)}, u32[]{:S(2)}, u32[]{:S(2)}) collective-permute-start(bf16[2,1,40,1920]{3,2,0,1:T(8,128)(2,1)S(1)} %get-tuple-element.111), channel_id=1, source_target_pairs={{0,16},{8,24},{16,0},{24,8},{1,17},{9,25},{17,1},{25,9},{2,18},{10... | collective-permute-start | bytes 921608 | tf_op jit(solution)/shard_map/ppermute | solution.py:237
  178.4 27.1 %collective-permute-start.31 = (bf16[2,1,40,1920]{3,2,0,1:T(8,128)(2,1)S(1)}, bf16[2,1,40,1920]{3,2,0,1:T(8,128)(2,1)S(1)}, u32[]{:S(2)}, u32[]{:S(2)}) collective-permute-start(bf16[2,1,40,1920]{3,2,0,1:T(8,128)(2,1)S(1)} %get-tuple-element.121), channel_id=1, source_target_pairs={{0,16},{8,24},{16,0},{24,8},{1,17},{9,25},{17,1},{25,9},{2,18},{10... | collective-permute-start | bytes 921608 | tf_op jit(solution)/shard_map/ppermute | solution.py:237
  180.0 31.2 %collective-permute-start.33 = (bf16[2,1,40,1920]{3,2,0,1:T(8,128)(2,1)S(1)}, bf16[2,1,40,1920]{3,2,0,1:T(8,128)(2,1)S(1)}, u32[]{:S(2)}, u32[]{:S(2)}) collective-permute-start(bf16[2,1,40,1920]{3,2,0,1:T(8,128)(2,1)S(1)} %get-tuple-element.123), channel_id=1, source_target_pairs={{0,16},{8,24},{16,0},{24,8},{1,17},{9,25},{17,1},{25,9},{2,18},{10... | collective-permute-start | bytes 921608 | tf_op jit(solution)/shard_map/ppermute | solution.py:237
  186.3 47.3 %collective-permute-start.22 = (bf16[80,1920]{1,0:T(8,128)(2,1)S(1)}, bf16[80,1920]{1,0:T(8,128)(2,1)S(1)}, u32[]{:S(2)}, u32[]{:S(2)}) collective-permute-start(bf16[80,1920]{1,0:T(8,128)(2,1)S(1)} %bitcast.160), channel_id=1, source_target_pairs={{0,3},{1,2},{2,1},{3,0},{4,7},{5,6},{6,5},{7,4},{8,11},{9,10},{10,... | collective-permute-start | bytes 921608 | tf_op jit(solution)/shard_map/ppermute | solution.py:234
  199.1 42.1 %collective-permute-start.24 = (bf16[80,1920]{1,0:T(8,128)(2,1)S(1)}, bf16[80,1920]{1,0:T(8,128)(2,1)S(1)}, u32[]{:S(2)}, u32[]{:S(2)}) collective-permute-start(bf16[80,1920]{1,0:T(8,128)(2,1)S(1)} %bitcast.161), channel_id=1, source_target_pairs={{0,5},{1,4},{2,7},{3,6},{4,1},{5,0},{6,3},{7,2},{8,13},{9,12},{10,... | collective-permute-start | bytes 921608 | tf_op jit(solution)/shard_map/ppermute | solution.py:234
  205.6 36.1 %collective-permute-start.32 = (bf16[80,1920]{1,0:T(8,128)(2,1)S(1)}, bf16[80,1920]{1,0:T(8,128)(2,1)S(1)}, u32[]{:S(2)}, u32[]{:S(2)}) collective-permute-start(bf16[80,1920]{1,0:T(8,128)(2,1)S(1)} %bitcast.162), channel_id=1, source_target_pairs={{0,6},{1,7},{2,4},{3,5},{4,2},{5,3},{6,0},{7,1},{8,14},{9,15},{10,... | collective-permute-start | bytes 921608 | tf_op jit(solution)/shard_map/ppermute | solution.py:234
  209.7 22.2 %collective-permute-start.10 = (bf16[2,2,40,1920]{3,2,0,1:T(8,128)(2,1)S(1)}, bf16[2,2,40,1920]{3,2,0,1:T(8,128)(2,1)S(1)}, u32[]{:S(2)}, u32[]{:S(2)}) collective-permute-start(bf16[2,2,40,1920]{3,2,0,1:T(8,128)(2,1)S(1)} %get-tuple-element.97), channel_id=1, source_target_pairs={{0,16},{8,24},{16,0},{24,8},{1,17},{9,25},{17,1},{25,9},{2,18},{10... | collective-permute-start | bytes 1843208 | tf_op jit(solution)/shard_map/ppermute | solution.py:237
  211.2 19.3 %collective-permute-start.13 = (bf16[2,1,40,1920]{3,2,0,1:T(8,128)(2,1)S(1)}, bf16[2,1,40,1920]{3,2,0,1:T(8,128)(2,1)S(1)}, u32[]{:S(2)}, u32[]{:S(2)}) collective-permute-start(bf16[2,1,40,1920]{3,2,0,1:T(8,128)(2,1)S(1)} %get-tuple-element.99), channel_id=1, source_target_pairs={{0,16},{8,24},{16,0},{24,8},{1,17},{9,25},{17,1},{25,9},{2,18},{10... | collective-permute-start | bytes 921608 | tf_op jit(solution)/shard_map/ppermute | solution.py:237
  230.4 21.8 %collective-permute-start.34 = (bf16[80,1920]{1,0:T(8,128)(2,1)S(1)}, bf16[80,1920]{1,0:T(8,128)(2,1)S(1)}, u32[]{:S(2)}, u32[]{:S(2)}) collective-permute-start(bf16[80,1920]{1,0:T(8,128)(2,1)S(1)} %bitcast.163), channel_id=1, source_target_pairs={{0,7},{1,6},{2,5},{3,4},{4,3},{5,2},{6,1},{7,0},{8,15},{9,14},{10,... | collective-permute-start | bytes 921608 | tf_op jit(solution)/shard_map/ppermute | solution.py:234
  231.9 20.4 %collective-permute-start.9 = (bf16[2,1,40,1920]{3,2,0,1:T(8,128)(2,1)S(1)}, bf16[2,1,40,1920]{3,2,0,1:T(8,128)(2,1)S(1)}, u32[]{:S(2)}, u32[]{:S(2)}) collective-permute-start(bf16[2,1,40,1920]{3,2,0,1:T(8,128)(2,1)S(1)} %get-tuple-element.95), channel_id=1, source_target_pairs={{0,16},{8,24},{16,0},{24,8},{1,17},{9,25},{17,1},{25,9},{2,18},{10... | collective-permute-start | bytes 921608 | tf_op jit(solution)/shard_map/ppermute | solution.py:237
  233.6 25.6 %collective-permute-start.14 = (bf16[80,1920]{1,0:T(8,128)(2,1)S(1)}, bf16[80,1920]{1,0:T(8,128)(2,1)S(1)}, u32[]{:S(2)}, u32[]{:S(2)}) collective-permute-start(bf16[80,1920]{1,0:T(8,128)(2,1)S(1)} %bitcast.164), channel_id=1, source_target_pairs={{0,4},{1,5},{2,6},{3,7},{4,0},{5,1},{6,2},{7,3},{8,12},{9,13},{10,... | collective-permute-start | bytes 921608 | tf_op jit(solution)/shard_map/ppermute | solution.py:234
  241.2 18.0 %collective-permute-start.11 = (bf16[80,1920]{1,0:T(8,128)(2,1)S(1)}, bf16[80,1920]{1,0:T(8,128)(2,1)S(1)}, u32[]{:S(2)}, u32[]{:S(2)}) collective-permute-start(bf16[80,1920]{1,0:T(8,128)(2,1)S(1)} %bitcast.159), channel_id=1, source_target_pairs={{0,1},{1,0},{2,3},{3,2},{4,5},{5,4},{6,7},{7,6},{8,9},{9,8},{10,11... | collective-permute-start | bytes 921608 | tf_op jit(solution)/shard_map/ppermute | solution.py:234
  (21 other events, 216.0 us)
